TPU v7x, 256 devices: a whole 4x4x8 slice. The times are simulated.
256 devices in a mesh: round: 2 (over x_hi), seq: 128 (over z, x_lo, y, core).
Axes of the slice: x: 4 (x_hi: 2, x_lo: 2; x = x_hi * 2 + x_lo), y: 4, z: 8, core: 2. Of those that a mesh axis runs over, the one named last changes fastest.
Arguments:
- qk: bfloat16 [65536, 1024], P('seq'), may hold values from -96 to 96
- values: bfloat16 [65536, 1024], P('seq'), may hold values from -6 to 6
- dest_dev: int32 [2, 65536], P('round', 'seq'), may hold values from 0 to 127, as said below
- dest_slot: int32 [2, 65536], P('round', 'seq'), may hold values from 0 to 511, as said below
Outputs:
- merged: bfloat16 [65536, 1024], P('seq', 'round')
Inputs may be any that keep to these rules, and one draw needn't show every extreme that they name: dest_dev and dest_slot together send each round's 65536 tokens to 65536 distinct positions. In each round, from the rows of one index of seq at most 6 go to any one index of seq, and exactly 6 for some pair; every index receives exactly 512 rows. `dest_slot`: the row within the destination's block, see dest_dev.
All inputs are finite; a program needn't handle non-finite values.
Results may differ from a plain program's by a relative error of at most 0.03.
Values may be sent and summed in bfloat16 or wider, within the bound.
No kernel may reach another device: no remote copies, remote signals or barrier semaphores. Data moves between devices by JAX's collectives and lax.ppermute only.
A program may use at most 64 MiB of HBM per device.

v0:
```python
import jax
import jax.numpy as jnp
from jax import lax
from jax.experimental import pallas as pl
from jax.experimental.pallas import tpu as pltpu
from jax.sharding import PartitionSpec as P


HEAD = 128
ROWS = 512
CAP = 6
UNIT = 8
HOPS = 4
PEERS = 32
STR = 4
PB = HOPS * CAP
MSG = STR * PB
SLOTS = PEERS * PB
PLACES = PEERS * STR * UNIT
EXTRA = 16
SIDE = 8
MSG_OUT = MSG + SIDE
QK_MAX = 96.0
PAD_MARK = 1024.0

eps_norm = 1e-06
self_score = -100000.0

bf16 = jnp.bfloat16
f32 = jnp.float32
i32 = jnp.int32


def iota(shape, dim):
    return lax.broadcasted_iota(i32, shape, dim)


def dot(a, b):
    return lax.dot_general(a, b, (((1,), (0,)), ((), ())), preferred_element_type=f32)


def dot_nt(a, b):
    return lax.dot_general(a, b, (((1,), (1,)), ((), ())), preferred_element_type=f32)


def ones_where(mask):
    return jnp.where(mask, 1.0, 0.0).astype(bf16)


def call(body, out_shape, scratch=(), **kw):
    return pl.pallas_call(
        body,
        out_shape=out_shape,
        scratch_shapes=list(scratch),
        compiler_params=pltpu.CompilerParams(vmem_limit_bytes=56 << 20),
        **kw,
    )


def store(ref, value):
    ref[...] = value


def each_peer(body, step=4):
    def some(i, carry):
        for n in range(step):
            body(i * step + n)
        return carry

    lax.fori_loop(0, PEERS // step, some, 0)


def place_rows(dest):
    col = jnp.broadcast_to(dest.astype(f32), (8, ROWS)).T[:, 0:1]
    same = col == dest.astype(f32)
    before = iota((ROWS, ROWS), 0) < iota((ROWS, ROWS), 1)
    rank = jnp.sum(jnp.where(same & before, 1.0, 0.0), axis=0, keepdims=True)
    pos = dest * UNIT + rank.astype(i32)
    high = pos >> 4
    low = pos - high * 16
    half = ROWS // 2
    parts = [x[:, h * half : (h + 1) * half] for h in range(2) for x in (high, low)]
    return jnp.concatenate(parts, axis=0).astype(f32)


def copy_all(copies):
    for c in copies:
        c.start()
    for c in copies:
        c.wait()


def lanes_of(spot):
    return pl.ds(pl.multiple_of(spot * HEAD, HEAD), HEAD)


def split_body(spot_ref, qk_ref, v_ref, *refs):
    outs, sems = refs[:HOPS], refs[HOPS]
    copies = []
    for o in range(HOPS):
        head = spot_ref[0] * HOPS + ((spot_ref[1] + o) & (HOPS - 1))
        for n, ref in enumerate((qk_ref, v_ref)):
            copies.append(
                pltpu.make_async_copy(
                    ref.at[:, lanes_of(head)],
                    outs[o].at[:, n * HEAD : (n + 1) * HEAD],
                    sems.at[o * 2 + n],
                )
            )
    copy_all(copies)


SMEM = pl.BlockSpec(memory_space=pltpu.SMEM)
HBM = pl.BlockSpec(memory_space=pl.ANY)


def split_heads(spot, qk, values):
    return call(
        split_body,
        (jax.ShapeDtypeStruct((ROWS, 2 * HEAD), bf16),) * HOPS,
        [pltpu.SemaphoreType.DMA((2 * HOPS,))],
        in_specs=[SMEM, HBM, HBM],
        name="split_heads",
    )(spot, qk, values)


def place_body(spot_ref, own_ref, other_ref, o_ref):
    own = place_rows(own_ref[...])
    other = place_rows(other_ref[...])
    mine = spot_ref[0] == 0
    o_ref[...] = jnp.concatenate(
        [jnp.where(mine, own, other), jnp.where(mine, other, own), jnp.zeros((8, ROWS // 2), f32)],
        axis=0,
    ).astype(bf16)


def places(spot, own, other):
    vmem = pl.BlockSpec(memory_space=pltpu.VMEM)
    return call(
        place_body,
        jax.ShapeDtypeStruct((EXTRA, 2 * HEAD), bf16),
        in_specs=[SMEM, vmem, vmem],
        name="places",
    )(spot, own, other)


def pack(xs, spots, r):
    def body(*refs):
        x_refs, e_refs = refs[:HOPS], refs[HOPS : 2 * HOPS]
        o_ref, pos_ref, acc_ref = refs[2 * HOPS :]
        ids = iota((PLACES, ROWS), 0)
        ones = jnp.full((ROWS, HEAD), 1.0, bf16)
        for j in range(HOPS):
            rows = e_refs[j][...].astype(f32)[4 * r : 4 * r + 4]
            pos = jnp.concatenate(
                [rows[0:1] * 16.0 + rows[1:2], rows[2:3] * 16.0 + rows[3:4]], axis=1
            ).astype(i32)
            pos_ref[j : j + 1, :] = pos
            pick = ones_where(pos == ids)
            got = dot(pick, x_refs[j][...])
            mark = (1.0 - dot(pick, ones)) * PAD_MARK
            left = (got[:, 0:HEAD] + mark).reshape(PEERS, STR, UNIT, HEAD)
            right = got[:, HEAD:].reshape(PEERS, STR, UNIT, HEAD)
            for q in range(STR):
                at = q * PB + j * CAP
                acc_ref[:, at : at + CAP, 0:HEAD] = left[:, q, 0:CAP, :]
                acc_ref[:, at : at + CAP, HEAD:] = right[:, q, 0:CAP, :]
        each_peer(lambda p: store(o_ref.at[p], acc_ref[p].astype(bf16)))

    shape = (PEERS, MSG, 2 * HEAD)
    return call(
        body,
        (jax.ShapeDtypeStruct(shape, bf16), jax.ShapeDtypeStruct((HOPS, ROWS), i32)),
        [pltpu.VMEM(shape, f32)],
        name="pack",
    )(*xs, *spots)


def tail_body(x_ref, o_ref):
    x = x_ref[...].astype(f32)[:, UNIT:, :].reshape(SLOTS, 2 * HEAD).astype(bf16)
    upper = ones_where(iota((SLOTS, SLOTS), 0) < iota((SLOTS, SLOTS), 1))
    first = ones_where(iota((8, HEAD), 1) == 0)
    ok = jnp.where(jnp.abs(dot_nt(first, x[:, 0:HEAD])) <= QK_MAX, 1.0, 0.0)
    row = jnp.where(ok > 0.0, dot(ok.astype(bf16), upper), -1.0).astype(i32)
    o_ref[...] = dot(ones_where(row[0:1, :] == iota((ROWS, SLOTS), 0)), x).astype(bf16)


def tail_of(x):
    return pl.pallas_call(
        tail_body,
        out_shape=jax.ShapeDtypeStruct((ROWS, 2 * HEAD), bf16),
        grid=(1,),
        in_specs=[pl.BlockSpec((PEERS, PB + UNIT, 2 * HEAD), lambda i: (0, 2, 0))],
        out_specs=pl.BlockSpec((ROWS, 2 * HEAD), lambda i: (0, 0)),
        name="tail",
    )(x)


def compact_body(x_ref, tail_ref, o_ref, tcol_ref):
    lower = ones_where(iota((SLOTS, SLOTS), 1) < iota((SLOTS, SLOTS), 0))
    first = ones_where(iota((8, HEAD), 1) == 0)
    lane = iota((SLOTS, HEAD), 1)
    sub = iota((8, SLOTS), 0)
    row_ok = jnp.zeros((8, SLOTS), f32)
    col_ok = jnp.zeros((SLOTS, HEAD), f32)
    parts = []
    for pair in range(STR // 2):
        both = x_ref[:, pair * 2 * PB : (pair + 1) * 2 * PB, :].astype(f32)
        for half in range(2):
            q = pair * 2 + half
            x = both[:, half * PB : (half + 1) * PB, :].reshape(SLOTS, 2 * HEAD)
            lead = jnp.broadcast_to(x[:, 0:1], (SLOTS, HEAD))
            col_ok = jnp.where((lane == q) & (jnp.abs(lead) <= QK_MAX), 1.0, col_ok)
            x = x.astype(bf16)
            ahead = dot_nt(first, x[:, 0:HEAD])
            row_ok = jnp.where((sub == q) & (jnp.abs(ahead) <= QK_MAX), 1.0, row_ok)
            parts.append(x)
    tcol_ref[...] = jnp.where(col_ok > 0.0, dot(lower, col_ok.astype(bf16)), -1.0)
    trow = jnp.where(row_ok > 0.0, dot_nt(row_ok.astype(bf16), lower), -1.0).astype(i32)
    ids = iota((ROWS, SLOTS), 0)
    for q in range(STR - 1):
        got = dot(ones_where(trow[q : q + 1, :] == ids), parts[q])
        o_ref[q * ROWS : (q + 1) * ROWS, :] = got.astype(bf16)
    o_ref[(STR - 1) * ROWS :, :] = tail_ref[...]


def compact(x, tail):
    return call(
        compact_body,
        (
            jax.ShapeDtypeStruct((STR * ROWS, 2 * HEAD), bf16),
            jax.ShapeDtypeStruct((SLOTS, HEAD), f32),
        ),
        name="compact",
    )(x, tail)


def unit(x):
    x = x.astype(f32)
    return (x * lax.rsqrt(jnp.sum(x * x, axis=1, keepdims=True) + eps_norm)).astype(bf16)


def attend_body(x_ref, halo_ref, tcol_ref, o_ref, out_ref, lse_ref, pk_ref, pv_ref):
    lse_ref[:, MSG:, :] = jnp.zeros((PEERS, HEAD - MSG, HEAD), f32)
    pk_ref[...] = unit(halo_ref[:, 0:HEAD])
    pv_ref[...] = halo_ref[:, HEAD:]

    def one(q, carry):
        here = pl.ds(pl.multiple_of(q * ROWS, ROWS), ROWS)
        qs = x_ref[here, 0:HEAD]
        vs = x_ref[here, HEAD:]
        ks = unit(qs)
        own = iota((ROWS, ROWS), 0) == iota((ROWS, ROWS), 1)
        sa = dot_nt(qs, pk_ref[...])
        sb = jnp.where(own, self_score, dot_nt(qs, ks))
        top = jnp.maximum(
            jnp.max(sa, axis=1, keepdims=True), jnp.max(sb, axis=1, keepdims=True)
        )
        pa = jnp.exp(sa - top)
        pb = jnp.exp(sb - top)
        total = jnp.sum(pa, axis=1, keepdims=True) + jnp.sum(pb, axis=1, keepdims=True)
        out = dot(pa.astype(bf16), pv_ref[...]) + dot(pb.astype(bf16), vs)
        lse = top + jnp.log(total)
        high = lse.astype(bf16).astype(f32)
        low = lse - high
        lane = iota((ROWS, HEAD), 1)
        side = jnp.where(lane == 0, high, jnp.where(lane == 1, low, 0.0))
        res = jnp.concatenate([(out / total).astype(bf16), side.astype(bf16)], axis=1)
        mine = iota((SLOTS, HEAD), 1) == q
        spots = jnp.sum(jnp.where(mine, tcol_ref[...], 0.0), axis=1, keepdims=True)
        got = dot(ones_where(spots.astype(i32) == iota((SLOTS, ROWS), 1)), res)
        at = pl.ds(pl.multiple_of(q * PB, UNIT), PB)
        out_ref[:, at, :] = got[:, 0:HEAD].reshape(PEERS, PB, HEAD)
        lse_ref[:, at, :] = got[:, HEAD:].reshape(PEERS, PB, HEAD)
        pk_ref[...] = ks
        pv_ref[...] = vs
        return carry

    lax.fori_loop(0, STR, one, 0)
    eye = ones_where(iota((SIDE, HEAD), 0) == iota((SIDE, HEAD), 1))

    def send(p):
        o_ref[p, 0:MSG, :] = out_ref[p].astype(bf16)
        o_ref[p, MSG:, :] = dot_nt(eye, lse_ref[p].astype(bf16)).astype(bf16)

    each_peer(send)


def attend(x, halo, tcol):
    return call(
        attend_body,
        jax.ShapeDtypeStruct((PEERS, MSG_OUT, HEAD), bf16),
        [
            pltpu.VMEM((PEERS, MSG, HEAD), f32),
            pltpu.VMEM((PEERS, HEAD, HEAD), f32),
            pltpu.VMEM((ROWS, HEAD), bf16),
            pltpu.VMEM((ROWS, HEAD), bf16),
        ],
        name="attend",
    )(x, halo, tcol)


def unpacked(pos, x_ref, acc_ref, slots):
    each_peer(lambda p: store(acc_ref.at[p], x_ref[p].astype(f32)))
    packed = acc_ref[:, MSG:, :].reshape(PEERS * SIDE, HEAD).astype(bf16)
    peer = pos >> 5
    rest = pos - (peer << 5)
    quarter = rest >> 3
    spot = quarter * PB + iota(pos.shape, 0) * CAP + rest - (quarter << 3)
    cols = jnp.concatenate([pos, peer, spot, spot], axis=0).astype(f32).T.astype(i32)
    lanes = iota((ROWS, PLACES), 1)
    spots = iota((ROWS, HEAD), 1)
    peers = iota((ROWS, PEERS * SIDE), 1) >> 3
    outs, lses = [], []
    for j in slots:
        pieces = [
            acc_ref[:, q * PB + j * CAP : q * PB + j * CAP + UNIT, :].reshape(PEERS, 1, UNIT, HEAD)
            for q in range(STR)
        ]
        rows = jnp.concatenate(pieces, axis=1).reshape(PLACES, HEAD).astype(bf16)
        outs.append(dot(ones_where(cols[:, j : j + 1] == lanes), rows))
        near = dot_nt(ones_where(cols[:, 8 + j : 9 + j] == spots), packed)
        mine = cols[:, 4 + j : 5 + j] == peers
        lses.append(jnp.sum(jnp.where(mine, near, 0.0), axis=1, keepdims=True))
    return outs, lses


def unpack_body(pos_ref, x_ref, o_ref, lse_ref, acc_ref):
    outs, lses = unpacked(pos_ref[...], x_ref, acc_ref, range(HOPS))
    lane = iota((ROWS, HEAD), 1)
    side = jnp.zeros((ROWS, HEAD), f32)
    for j in range(HOPS):
        o_ref[j] = outs[j].astype(bf16)
        side = jnp.where(lane == j, lses[j], side)
    lse_ref[...] = side


ACC = (PEERS, MSG_OUT, HEAD)
HEADS_OUT = (HOPS, ROWS, HEAD)


def unpack(pos, x):
    return call(
        unpack_body,
        (jax.ShapeDtypeStruct(HEADS_OUT, bf16), jax.ShapeDtypeStruct((ROWS, HEAD), f32)),
        [pltpu.VMEM(ACC, f32)],
        name="unpack",
    )(pos, x)


def merge(pos, x, other, other_lse, slots):
    def body(pos_ref, x_ref, other_ref, other_lse_ref, *refs):
        outs, lses = unpacked(pos_ref[...], x_ref, refs[-1], slots)
        for n, j in enumerate(slots):
            la, lb = other_lse_ref[:, j : j + 1], lses[n]
            top = jnp.maximum(la, lb)
            ea, eb = jnp.exp(la - top), jnp.exp(lb - top)
            mix = ea * other_ref[j].astype(f32) + eb * outs[n]
            refs[n][...] = (mix / (ea + eb)).astype(bf16)

    return call(
        body,
        (jax.ShapeDtypeStruct((ROWS, HEAD), bf16),) * len(slots),
        [pltpu.VMEM(ACC, f32)],
        name="merge",
    )(pos, x, other, other_lse)


def join_body(spot_ref, *refs):
    parts, o_ref = refs[:HOPS], refs[HOPS]
    for o in range(HOPS):
        head = (spot_ref[1] + o) & (HOPS - 1)
        o_ref[:, lanes_of(head)] = parts[o][...]


def join_heads(spot, parts):
    vmem = pl.BlockSpec(memory_space=pltpu.VMEM)
    return call(
        join_body,
        jax.ShapeDtypeStruct((ROWS, HOPS * HEAD), bf16),
        in_specs=[SMEM] + [vmem] * HOPS,
        name="join_heads",
    )(spot, *parts)


NEAR = [[PEERS * j + p for p in range(PEERS)] for j in range(HOPS)]
NEXT = [(PEERS * j + p, PEERS * j + (p + 1) % PEERS) for j in range(HOPS) for p in range(PEERS)]
ORDER = (2, 1, 3)


def hop(x, o):
    count = PEERS * HOPS
    return lax.ppermute(x, "seq", [(s, (s + PEERS * o) % count) for s in range(count)])


def swap(x):
    return lax.all_to_all(x, "seq", 0, 0, tiled=True, axis_index_groups=NEAR)


def on_device(qk, values, dest_dev, dest_slot):
    return routed(qk, values, dest_dev)


def routed(qk, values, dest_dev):
    spot = jnp.stack([lax.axis_index("round"), lax.axis_index("seq") // PEERS]).astype(i32)
    other = lax.ppermute(dest_dev, "round", [(0, 1), (1, 0)])
    mine = list(split_heads(spot, qk, values))
    for o in ORDER:
        mine[o] = hop(mine[o], o)
    here = places(spot, dest_dev, other)
    spots = [here] + [hop(here, o) for o in range(1, HOPS)]
    sent, pos = zip(*[pack(mine, spots, r) for r in range(2)])
    got = [swap(sent[0])]
    tails = [tail_of(got[0])]
    halo = lax.ppermute(tails[0], "seq", NEXT)
    got.append(swap(sent[1]))
    reply = attend(*arranged(got[0], tails[0], halo))
    tails.append(tail_of(got[1]))
    halo = lax.ppermute(tails[1], "seq", NEXT)
    back = [swap(reply)]
    back.append(swap(attend(*arranged(got[1], tails[1], halo))))
    out, lse = unpack(pos[0], back[0])
    done = {}
    done[2], done[1] = merge(pos[1], back[1], out, lse, (2, 1))
    for o in (2, 1):
        done[o] = hop(done[o], -o)
    done[3], done[0] = merge(pos[1], back[1], out, lse, (3, 0))
    done[3] = hop(done[3], -3)
    return join_heads(spot, [done[o] for o in range(HOPS)])


def arranged(got, tail, halo):
    rows, tcol = compact(got, tail)
    return rows, halo, tcol


def solution(mesh):
    return jax.shard_map(
        on_device,
        mesh=mesh,
        in_specs=(P("seq", None), P("seq", None), P("round", "seq"), P("round", "seq")),
        out_specs=P("seq", "round"),
        check_vma=False,
    )
```

profile of v0, /device:TPU:4, one launch (start us, length us, event | category | flops | bytes accessed | tf_op | source)
XLA Modules:
  0.0 194.7 jit_solution(7608325977037179916)
XLA Ops:
  0.0 0.6 pad_add_fusion.spot_ref
  0.6 3.0 %split_heads.1 = (bf16[512,256]{1,0:T(8,128)(2,1)}, bf16[512,256]{1,0:T(8,128)(2,1)}, bf16[512,256]{1,0:T(8,128)(2,1)}, bf16[512,256]{1,0:T(8,128)(2,1)}) custom-call(s32[2]{0:T(128)} %pad_add_fusion.spot_ref, bf16[512,1024]{1,0:T(8,128)(2,1)} %qk_ref.1, bf16[512,1024]{1,0:T(8,128)(2,1)} %v_ref.1), custom_call_target="tpu_custom_call" | custom-call | tf_op jit(solution)/shard_map/split_heads/pallas_call | solution.py:118
  3.6 3.3 %collective-permute-start = (bf16[512,256]{1,0:T(8,128)(2,1)}, bf16[512,256]{1,0:T(8,128)(2,1)S(1)}, u32[]{:S(2)}, u32[]{:S(2)}) collective-permute-start(bf16[512,256]{1,0:T(8,128)(2,1)} %get-tuple-element.24), channel_id=1, source_target_pairs={{0,32},{1,33},{2,34},{3,35},{4,36},{5,37},{6,38},{7,39},{8,40},{9,... | collective-permute-start | bytes 786440 | tf_op jit(solution)/shard_map/ppermute | solution.py:393
  6.9 5.4 %collective-permute-start.1 = (bf16[512,256]{1,0:T(8,128)(2,1)}, bf16[512,256]{1,0:T(8,128)(2,1)S(1)}, u32[]{:S(2)}, u32[]{:S(2)}) collective-permute-start(bf16[512,256]{1,0:T(8,128)(2,1)} %get-tuple-element.25), channel_id=1, source_target_pairs={{0,64},{1,65},{2,66},{3,67},{4,68},{5,69},{6,70},{7,71},{8,72},{9,... | collective-permute-start | bytes 786440 | tf_op jit(solution)/shard_map/ppermute | solution.py:393
  12.3 2.7 %collective-permute-start.2 = (bf16[512,256]{1,0:T(8,128)(2,1)}, bf16[512,256]{1,0:T(8,128)(2,1)S(1)}, u32[]{:S(2)}, u32[]{:S(2)}) collective-permute-start(bf16[512,256]{1,0:T(8,128)(2,1)} %get-tuple-element.26), channel_id=1, source_target_pairs={{0,96},{1,97},{2,98},{3,99},{4,100},{5,101},{6,102},{7,103},{8,104... | collective-permute-start | bytes 786440 | tf_op jit(solution)/shard_map/ppermute | solution.py:393
  15.0 0.0 copy-done.15
  15.0 0.5 collective-permute-start.3
  15.5 4.6 %collective-permute-done.3.other_ref = s32[1,512]{1,0:T(1,128)S(1)} collective-permute-done((s32[1,512]{1,0:T(1,128)S(1)}, s32[1,512]{1,0:T(1,128)S(1)}, u32[]{:S(2)}, u32[]{:S(2)}) %collective-permute-start.3) | collective-permute-done | bytes 2080 | tf_op jit(solution)/shard_map/ppermute | solution.py:406
  20.1 0.6 copy-done.16
  20.6 1.7 places.1.refs_4_
  22.4 0.0 collective-permute-start.6
  22.4 3.8 %collective-permute-start.5 = (bf16[16,256]{1,0:T(8,128)(2,1)}, bf16[16,256]{1,0:T(8,128)(2,1)S(1)}, u32[]{:S(2)}, u32[]{:S(2)}) collective-permute-start(bf16[16,256]{1,0:T(8,128)(2,1)} %places.1.refs_4_), channel_id=1, source_target_pairs={{0,64},{1,65},{2,66},{3,67},{4,68},{5,69},{6,70},{7,71},{8,72},{9,... | collective-permute-start | bytes 24584 | tf_op jit(solution)/shard_map/ppermute | solution.py:393
  26.2 10.5 %collective-permute-done.6.refs_7_ = bf16[16,256]{1,0:T(8,128)(2,1)S(1)} collective-permute-done((bf16[16,256]{1,0:T(8,128)(2,1)}, bf16[16,256]{1,0:T(8,128)(2,1)S(1)}, u32[]{:S(2)}, u32[]{:S(2)}) %collective-permute-start.6) | collective-permute-done | bytes 8224 | tf_op jit(solution)/shard_map/ppermute | solution.py:393
  36.8 1.5 collective-permute-start.4
  38.3 0.0 collective-permute-done.5.refs_6_
  38.3 4.4 %collective-permute-done.4.refs_5_ = bf16[16,256]{1,0:T(8,128)(2,1)S(1)} collective-permute-done((bf16[16,256]{1,0:T(8,128)(2,1)}, bf16[16,256]{1,0:T(8,128)(2,1)S(1)}, u32[]{:S(2)}, u32[]{:S(2)}) %collective-permute-start.4) | collective-permute-done | bytes 8224 | tf_op jit(solution)/shard_map/ppermute | solution.py:393
  42.7 0.0 collective-permute-done.refs_1_
  42.7 0.0 collective-permute-done.1.refs_2_
  42.7 0.0 copy-start.5
  42.7 0.0 collective-permute-done.2.refs_3_
  42.8 0.0 copy-start.6
  42.8 0.0 copy-done.12
  42.8 0.0 copy-done.13
  42.8 0.5 copy-done.14
  43.3 0.1 copy-done.4
  43.5 0.1 copy-done.5
  43.5 0.1 copy-done.6
  43.6 4.9 %pack.3 = (bf16[32,96,256]{2,1,0:T(8,128)(2,1)}, s32[4,512]{1,0:T(4,128)}) custom-call(bf16[512,256]{1,0:T(8,128)(2,1)} %get-tuple-element.23.refs_0_, bf16[512,256]{1,0:T(8,128)(2,1)} %copy-done.4, bf16[512,256]{1,0:T(8,128)(2,1)} %copy-done.5, bf16[512,256]{1,0:T(8,128)(2,1)} %copy-done.6, bf16[16,256]{1,0:T(8,128)(2,1)} %places.1.refs_4_, ...), custom_call_target="tpu_custom_call" | custom-call | tf_op jit(solution)/shard_map/pack/pallas_call | solution.py:171
  48.5 5.5 %all-to-all-start.2 = ((bf16[32,96,256]{2,1,0:T(8,128)(2,1)}), bf16[32,96,256]{2,1,0:T(8,128)(2,1)S(1)}, u32[]{:S(2)}, u32[]{:S(2)}) async-start(bf16[32,96,256]{2,1,0:T(8,128)(2,1)} %get-tuple-element.32), calls=%async_computation.2 | async-start | bytes 3145728 | tf_op jit(solution)/shard_map/all_to_all | solution.py:397
  54.0 4.9 %pack.2 = (bf16[32,96,256]{2,1,0:T(8,128)(2,1)}, s32[4,512]{1,0:T(4,128)}) custom-call(bf16[512,256]{1,0:T(8,128)(2,1)} %get-tuple-element.23.refs_0_, bf16[512,256]{1,0:T(8,128)(2,1)} %copy-done.4, bf16[512,256]{1,0:T(8,128)(2,1)} %copy-done.5, bf16[512,256]{1,0:T(8,128)(2,1)} %copy-done.6, bf16[16,256]{1,0:T(8,128)(2,1)} %places.1.refs_4_, ...), custom_call_target="tpu_custom_call" | custom-call | tf_op jit(solution)/shard_map/pack/pallas_call | solution.py:171
  58.9 16.7 %all-to-all-done.2.x_ref = bf16[32,96,256]{2,1,0:T(8,128)(2,1)S(1)} async-done(((bf16[32,96,256]{2,1,0:T(8,128)(2,1)}), bf16[32,96,256]{2,1,0:T(8,128)(2,1)S(1)}, u32[]{:S(2)}, u32[]{:S(2)}) %all-to-all-start.2) | async-done | bytes 1572896 | tf_op jit(solution)/shard_map/all_to_all | solution.py:397
  75.7 1.2 copy-done.1
  76.8 4.3 %all-to-all-start = ((bf16[32,96,256]{2,1,0:T(8,128)(2,1)}), bf16[32,96,256]{2,1,0:T(8,128)(2,1)S(1)}, u32[]{:S(2)}, u32[]{:S(2)}) async-start(bf16[32,96,256]{2,1,0:T(8,128)(2,1)} %get-tuple-element.28), calls=%async_computation | async-start | bytes 3145728 | tf_op jit(solution)/shard_map/all_to_all | solution.py:397
  81.1 2.4 %tail.3.tail_ref = bf16[512,256]{1,0:T(8,128)(2,1)} custom-call(bf16[32,96,256]{2,1,0:T(8,128)(2,1)} %copy-done.1), custom_call_target="tpu_custom_call" | custom-call | tf_op jit(solution)/shard_map/tail/pallas_call | solution.py:189
  83.6 0.3 collective-permute-start.8
  83.9 4.0 %compact.3 = (bf16[2048,256]{1,0:T(8,128)(2,1)}, f32[768,128]{1,0:T(8,128)}) custom-call(bf16[32,96,256]{2,1,0:T(8,128)(2,1)} %copy-done.1, bf16[512,256]{1,0:T(8,128)(2,1)} %tail.3.tail_ref), custom_call_target="tpu_custom_call" | custom-call | tf_op jit(solution)/shard_map/compact/pallas_call | solution.py:228
  87.9 18.9 %collective-permute-done.8.halo_ref = bf16[512,256]{1,0:T(8,128)(2,1)S(1)} collective-permute-done((bf16[512,256]{1,0:T(8,128)(2,1)}, bf16[512,256]{1,0:T(8,128)(2,1)S(1)}, u32[]{:S(2)}, u32[]{:S(2)}) %collective-permute-start.8) | collective-permute-done | bytes 262176 | tf_op jit(solution)/shard_map/ppermute | solution.py:415
  106.8 0.7 copy-done.7
  107.5 10.7 %attend.3 = bf16[32,104,128]{2,1,0:T(8,128)(2,1)} custom-call(bf16[2048,256]{1,0:T(8,128)(2,1)} %get-tuple-element.33.x_ref, bf16[512,256]{1,0:T(8,128)(2,1)} %copy-done.7, f32[768,128]{1,0:T(8,128)} %get-tuple-element.34.tcol_ref), custom_call_target="tpu_custom_call" | custom-call | tf_op jit(solution)/shard_map/attend/pallas_call | solution.py:290
  118.2 0.0 all-to-all-done.x_ref
  118.2 3.9 %all-to-all-start.3 = ((bf16[32,104,128]{2,1,0:T(8,128)(2,1)}), bf16[32,104,128]{2,1,0:T(8,128)(2,1)S(1)}, u32[]{:S(2)}, u32[]{:S(2)}) async-start(bf16[32,104,128]{2,1,0:T(8,128)(2,1)} %attend.3), calls=%async_computation.3 | async-start | bytes 1703936 | tf_op jit(solution)/shard_map/all_to_all | solution.py:397
  122.1 0.0 copy-done
  122.2 2.4 %tail.2.tail_ref = bf16[512,256]{1,0:T(8,128)(2,1)} custom-call(bf16[32,96,256]{2,1,0:T(8,128)(2,1)} %copy-done), custom_call_target="tpu_custom_call" | custom-call | tf_op jit(solution)/shard_map/tail/pallas_call | solution.py:189
  124.6 0.2 collective-permute-start.7
  124.7 4.0 %compact.2 = (bf16[2048,256]{1,0:T(8,128)(2,1)}, f32[768,128]{1,0:T(8,128)}) custom-call(bf16[32,96,256]{2,1,0:T(8,128)(2,1)} %copy-done, bf16[512,256]{1,0:T(8,128)(2,1)} %tail.2.tail_ref), custom_call_target="tpu_custom_call" | custom-call | tf_op jit(solution)/shard_map/compact/pallas_call | solution.py:228
  128.8 11.3 %collective-permute-done.7.halo_ref = bf16[512,256]{1,0:T(8,128)(2,1)S(1)} collective-permute-done((bf16[512,256]{1,0:T(8,128)(2,1)}, bf16[512,256]{1,0:T(8,128)(2,1)S(1)}, u32[]{:S(2)}, u32[]{:S(2)}) %collective-permute-start.7) | collective-permute-done | bytes 262176 | tf_op jit(solution)/shard_map/ppermute | solution.py:419
  140.0 0.7 copy-done.8
  140.7 10.7 %attend.2 = bf16[32,104,128]{2,1,0:T(8,128)(2,1)} custom-call(bf16[2048,256]{1,0:T(8,128)(2,1)} %get-tuple-element.29.x_ref, bf16[512,256]{1,0:T(8,128)(2,1)} %copy-done.8, f32[768,128]{1,0:T(8,128)} %get-tuple-element.30.tcol_ref), custom_call_target="tpu_custom_call" | custom-call | tf_op jit(solution)/shard_map/attend/pallas_call | solution.py:290
  151.4 0.0 all-to-all-done.3.x_ref
  151.4 4.1 %all-to-all-start.1 = ((bf16[32,104,128]{2,1,0:T(8,128)(2,1)}), bf16[32,104,128]{2,1,0:T(8,128)(2,1)S(1)}, u32[]{:S(2)}, u32[]{:S(2)}) async-start(bf16[32,104,128]{2,1,0:T(8,128)(2,1)} %attend.2), calls=%async_computation.1 | async-start | bytes 1703936 | tf_op jit(solution)/shard_map/all_to_all | solution.py:397
  155.6 4.4 %unpack.1 = (bf16[4,512,128]{2,1,0:T(8,128)(2,1)}, f32[512,128]{1,0:T(8,128)}) custom-call(s32[4,512]{1,0:T(4,128)} %get-tuple-element.31.pos_ref, bf16[32,104,128]{2,1,0:T(8,128)(2,1)} %copy-done.3), custom_call_target="tpu_custom_call" | custom-call | tf_op jit(solution)/shard_map/unpack/pallas_call | solution.py:343
  160.0 9.6 %all-to-all-done.1.x_ref = bf16[32,104,128]{2,1,0:T(8,128)(2,1)S(1)} async-done(((bf16[32,104,128]{2,1,0:T(8,128)(2,1)}), bf16[32,104,128]{2,1,0:T(8,128)(2,1)S(1)}, u32[]{:S(2)}, u32[]{:S(2)}) %all-to-all-start.1) | async-done | bytes 852000 | tf_op jit(solution)/shard_map/all_to_all | solution.py:397
  169.6 0.9 copy-done.2
  170.5 4.7 %merge.3 = (bf16[512,128]{1,0:T(8,128)(2,1)}, bf16[512,128]{1,0:T(8,128)(2,1)}) custom-call(s32[4,512]{1,0:T(4,128)} %get-tuple-element.27.pos_ref, bf16[32,104,128]{2,1,0:T(8,128)(2,1)} %copy-done.2, bf16[4,512,128]{2,1,0:T(8,128)(2,1)} %get-tuple-element.35.other_ref, f32[512,128]{1,0:T(8,128)} %get-tuple-element.36.other_lse_ref), custom_call_target="tpu_custom_call" | custom-call | tf_op jit(solution)/shard_map/merge/pallas_call | solution.py:361
  175.2 2.3 %collective-permute-start.9 = (bf16[512,128]{1,0:T(8,128)(2,1)}, bf16[512,128]{1,0:T(8,128)(2,1)S(1)}, u32[]{:S(2)}, u32[]{:S(2)}) collective-permute-start(bf16[512,128]{1,0:T(8,128)(2,1)} %get-tuple-element.38), channel_id=1, source_target_pairs={{0,96},{1,97},{2,98},{3,99},{4,100},{5,101},{6,102},{7,103},{8,104... | collective-permute-start | bytes 393224 | tf_op jit(solution)/shard_map/ppermute | solution.py:393
  177.5 1.9 collective-permute-start.10
  179.4 4.7 %merge.2 = (bf16[512,128]{1,0:T(8,128)(2,1)}, bf16[512,128]{1,0:T(8,128)(2,1)}) custom-call(s32[4,512]{1,0:T(4,128)} %get-tuple-element.27.pos_ref, bf16[32,104,128]{2,1,0:T(8,128)(2,1)} %copy-done.2, bf16[4,512,128]{2,1,0:T(8,128)(2,1)} %get-tuple-element.35.other_ref, f32[512,128]{1,0:T(8,128)} %get-tuple-element.36.other_lse_ref), custom_call_target="tpu_custom_call" | custom-call | tf_op jit(solution)/shard_map/merge/pallas_call | solution.py:361
  184.1 2.9 %collective-permute-start.11 = (bf16[512,128]{1,0:T(8,128)(2,1)}, bf16[512,128]{1,0:T(8,128)(2,1)S(1)}, u32[]{:S(2)}, u32[]{:S(2)}) collective-permute-start(bf16[512,128]{1,0:T(8,128)(2,1)} %get-tuple-element.40), channel_id=1, source_target_pairs={{0,32},{1,33},{2,34},{3,35},{4,36},{5,37},{6,38},{7,39},{8,40},{9,... | collective-permute-start | bytes 393224 | tf_op jit(solution)/shard_map/ppermute | solution.py:393
  187.1 0.0 collective-permute-done.9.refs_1_
  187.1 0.2 collective-permute-done.10.refs_2_
  187.3 4.8 %collective-permute-done.11.refs_3_ = bf16[512,128]{1,0:T(8,128)(2,1)S(1)} collective-permute-done((bf16[512,128]{1,0:T(8,128)(2,1)}, bf16[512,128]{1,0:T(8,128)(2,1)S(1)}, u32[]{:S(2)}, u32[]{:S(2)}) %collective-permute-start.11) | collective-permute-done | bytes 131104 | tf_op jit(solution)/shard_map/ppermute | solution.py:393
  192.0 0.0 copy-done.9
  192.0 0.7 copy-done.11
  192.7 2.0 %join_heads.1 = bf16[512,512]{1,0:T(8,128)(2,1)} custom-call(s32[2]{0:T(128)} %pad_add_fusion.spot_ref, bf16[512,128]{1,0:T(8,128)(2,1)} %get-tuple-element.37.refs_0_, bf16[512,128]{1,0:T(8,128)(2,1)} %copy-done.9, bf16[512,128]{1,0:T(8,128)(2,1)} %copy-done.10, bf16[512,128]{1,0:T(8,128)(2,1)} %copy-done.11), custom_call_target="tpu_custom_call" | custom-call | tf_op jit(solution)/shard_map/join_heads/pallas_call | solution.py:378
  (17 shorter events, 0.0 us)
Async XLA Ops:
  0.0 15.0 %copy-start.15 = (s32[1,512]{1,0:T(1,128)S(1)}, s32[1,512]{1,0:T(1,128)}, u32[]{:S(2)}) copy-start(s32[1,512]{1,0:T(1,128)} %own_ref.1) | copy-start | bytes 6148
  3.6 39.1 %collective-permute-start = (bf16[512,256]{1,0:T(8,128)(2,1)}, bf16[512,256]{1,0:T(8,128)(2,1)S(1)}, u32[]{:S(2)}, u32[]{:S(2)}) collective-permute-start(bf16[512,256]{1,0:T(8,128)(2,1)} %get-tuple-element.24), channel_id=1, source_target_pairs={{0,32},{1,33},{2,34},{3,35},{4,36},{5,37},{6,38},{7,39},{8,40},{9,... | collective-permute-start | bytes 786440 | tf_op jit(solution)/shard_map/ppermute | solution.py:393
  6.9 35.8 %collective-permute-start.1 = (bf16[512,256]{1,0:T(8,128)(2,1)}, bf16[512,256]{1,0:T(8,128)(2,1)S(1)}, u32[]{:S(2)}, u32[]{:S(2)}) collective-permute-start(bf16[512,256]{1,0:T(8,128)(2,1)} %get-tuple-element.25), channel_id=1, source_target_pairs={{0,64},{1,65},{2,66},{3,67},{4,68},{5,69},{6,70},{7,71},{8,72},{9,... | collective-permute-start | bytes 786440 | tf_op jit(solution)/shard_map/ppermute | solution.py:393
  12.3 30.4 %collective-permute-start.2 = (bf16[512,256]{1,0:T(8,128)(2,1)}, bf16[512,256]{1,0:T(8,128)(2,1)S(1)}, u32[]{:S(2)}, u32[]{:S(2)}) collective-permute-start(bf16[512,256]{1,0:T(8,128)(2,1)} %get-tuple-element.26), channel_id=1, source_target_pairs={{0,96},{1,97},{2,98},{3,99},{4,100},{5,101},{6,102},{7,103},{8,104... | collective-permute-start | bytes 786440 | tf_op jit(solution)/shard_map/ppermute | solution.py:393
  15.0 5.1 %collective-permute-start.3 = (s32[1,512]{1,0:T(1,128)S(1)}, s32[1,512]{1,0:T(1,128)S(1)}, u32[]{:S(2)}, u32[]{:S(2)}) collective-permute-start(s32[1,512]{1,0:T(1,128)S(1)} %copy-done.15), channel_id=1, source_target_pairs={{0,128},{128,0},{1,129},{129,1},{2,130},{130,2},{3,131},{131,3},{4... | collective-permute-start | bytes 6152 | tf_op jit(solution)/shard_map/ppermute | solution.py:406
  20.1 0.6 copy-start.16
  22.4 14.4 %collective-permute-start.6 = (bf16[16,256]{1,0:T(8,128)(2,1)}, bf16[16,256]{1,0:T(8,128)(2,1)S(1)}, u32[]{:S(2)}, u32[]{:S(2)}) collective-permute-start(bf16[16,256]{1,0:T(8,128)(2,1)} %places.1.refs_4_), channel_id=1, source_target_pairs={{0,96},{1,97},{2,98},{3,99},{4,100},{5,101},{6,102},{7,103},{8,104... | collective-permute-start | bytes 24584 | tf_op jit(solution)/shard_map/ppermute | solution.py:393
  22.4 15.9 %collective-permute-start.5 = (bf16[16,256]{1,0:T(8,128)(2,1)}, bf16[16,256]{1,0:T(8,128)(2,1)S(1)}, u32[]{:S(2)}, u32[]{:S(2)}) collective-permute-start(bf16[16,256]{1,0:T(8,128)(2,1)} %places.1.refs_4_), channel_id=1, source_target_pairs={{0,64},{1,65},{2,66},{3,67},{4,68},{5,69},{6,70},{7,71},{8,72},{9,... | collective-permute-start | bytes 24584 | tf_op jit(solution)/shard_map/ppermute | solution.py:393
  36.8 6.0 %copy-start.12 = (bf16[16,256]{1,0:T(8,128)(2,1)}, bf16[16,256]{1,0:T(8,128)(2,1)S(1)}, u32[]{:S(2)}) copy-start(bf16[16,256]{1,0:T(8,128)(2,1)S(1)} %collective-permute-done.6.refs_7_) | copy-start | bytes 24580
  36.8 6.0 %collective-permute-start.4 = (bf16[16,256]{1,0:T(8,128)(2,1)}, bf16[16,256]{1,0:T(8,128)(2,1)S(1)}, u32[]{:S(2)}, u32[]{:S(2)}) collective-permute-start(bf16[16,256]{1,0:T(8,128)(2,1)} %places.1.refs_4_), channel_id=1, source_target_pairs={{0,32},{1,33},{2,34},{3,35},{4,36},{5,37},{6,38},{7,39},{8,40},{9,... | collective-permute-start | bytes 24584 | tf_op jit(solution)/shard_map/ppermute | solution.py:393
  38.3 4.5 %copy-start.13 = (bf16[16,256]{1,0:T(8,128)(2,1)}, bf16[16,256]{1,0:T(8,128)(2,1)S(1)}, u32[]{:S(2)}) copy-start(bf16[16,256]{1,0:T(8,128)(2,1)S(1)} %collective-permute-done.5.refs_6_) | copy-start | bytes 24580
  42.7 0.6 copy-start.14
  42.7 0.7 copy-start.4
  42.7 0.8 copy-start.5
  42.8 0.8 copy-start.6
  48.5 27.2 %all-to-all-start.2 = ((bf16[32,96,256]{2,1,0:T(8,128)(2,1)}), bf16[32,96,256]{2,1,0:T(8,128)(2,1)S(1)}, u32[]{:S(2)}, u32[]{:S(2)}) async-start(bf16[32,96,256]{2,1,0:T(8,128)(2,1)} %get-tuple-element.32), calls=%async_computation.2 | async-start | bytes 3145728 | tf_op jit(solution)/shard_map/all_to_all | solution.py:397
  75.7 1.2 copy-start.1
  76.8 41.4 %all-to-all-start = ((bf16[32,96,256]{2,1,0:T(8,128)(2,1)}), bf16[32,96,256]{2,1,0:T(8,128)(2,1)S(1)}, u32[]{:S(2)}, u32[]{:S(2)}) async-start(bf16[32,96,256]{2,1,0:T(8,128)(2,1)} %get-tuple-element.28), calls=%async_computation | async-start | bytes 3145728 | tf_op jit(solution)/shard_map/all_to_all | solution.py:397
  83.6 23.3 %collective-permute-start.8 = (bf16[512,256]{1,0:T(8,128)(2,1)}, bf16[512,256]{1,0:T(8,128)(2,1)S(1)}, u32[]{:S(2)}, u32[]{:S(2)}) collective-permute-start(bf16[512,256]{1,0:T(8,128)(2,1)} %tail.3.tail_ref), channel_id=1, source_target_pairs={{0,1},{1,2},{2,3},{3,4},{4,5},{5,6},{6,7},{7,8},{8,9},{9,10},{10,1... | collective-permute-start | bytes 786440 | tf_op jit(solution)/shard_map/ppermute | solution.py:415
  106.8 0.7 copy-start.7
  118.2 3.9 %copy-start = (bf16[32,96,256]{2,1,0:T(8,128)(2,1)}, bf16[32,96,256]{2,1,0:T(8,128)(2,1)S(1)}, u32[]{:S(2)}) copy-start(bf16[32,96,256]{2,1,0:T(8,128)(2,1)S(1)} %all-to-all-done.x_ref) | copy-start | bytes 4718596
  118.2 33.2 %all-to-all-start.3 = ((bf16[32,104,128]{2,1,0:T(8,128)(2,1)}), bf16[32,104,128]{2,1,0:T(8,128)(2,1)S(1)}, u32[]{:S(2)}, u32[]{:S(2)}) async-start(bf16[32,104,128]{2,1,0:T(8,128)(2,1)} %attend.3), calls=%async_computation.3 | async-start | bytes 1703936 | tf_op jit(solution)/shard_map/all_to_all | solution.py:397
  124.6 15.4 %collective-permute-start.7 = (bf16[512,256]{1,0:T(8,128)(2,1)}, bf16[512,256]{1,0:T(8,128)(2,1)S(1)}, u32[]{:S(2)}, u32[]{:S(2)}) collective-permute-start(bf16[512,256]{1,0:T(8,128)(2,1)} %tail.2.tail_ref), channel_id=1, source_target_pairs={{0,1},{1,2},{2,3},{3,4},{4,5},{5,6},{6,7},{7,8},{8,9},{9,10},{10,1... | collective-permute-start | bytes 786440 | tf_op jit(solution)/shard_map/ppermute | solution.py:419
  140.0 0.7 copy-start.8
  151.4 4.1 %copy-start.3 = (bf16[32,104,128]{2,1,0:T(8,128)(2,1)}, bf16[32,104,128]{2,1,0:T(8,128)(2,1)S(1)}, u32[]{:S(2)}) copy-start(bf16[32,104,128]{2,1,0:T(8,128)(2,1)S(1)} %all-to-all-done.3.x_ref) | copy-start | bytes 2555908
  151.4 18.2 %all-to-all-start.1 = ((bf16[32,104,128]{2,1,0:T(8,128)(2,1)}), bf16[32,104,128]{2,1,0:T(8,128)(2,1)S(1)}, u32[]{:S(2)}, u32[]{:S(2)}) async-start(bf16[32,104,128]{2,1,0:T(8,128)(2,1)} %attend.2), calls=%async_computation.1 | async-start | bytes 1703936 | tf_op jit(solution)/shard_map/all_to_all | solution.py:397
  169.6 0.9 copy-start.2
  175.2 11.8 %collective-permute-start.9 = (bf16[512,128]{1,0:T(8,128)(2,1)}, bf16[512,128]{1,0:T(8,128)(2,1)S(1)}, u32[]{:S(2)}, u32[]{:S(2)}) collective-permute-start(bf16[512,128]{1,0:T(8,128)(2,1)} %get-tuple-element.38), channel_id=1, source_target_pairs={{0,96},{1,97},{2,98},{3,99},{4,100},{5,101},{6,102},{7,103},{8,104... | collective-permute-start | bytes 393224 | tf_op jit(solution)/shard_map/ppermute | solution.py:393
  177.5 9.7 %collective-permute-start.10 = (bf16[512,128]{1,0:T(8,128)(2,1)}, bf16[512,128]{1,0:T(8,128)(2,1)S(1)}, u32[]{:S(2)}, u32[]{:S(2)}) collective-permute-start(bf16[512,128]{1,0:T(8,128)(2,1)} %get-tuple-element.39), channel_id=1, source_target_pairs={{0,64},{1,65},{2,66},{3,67},{4,68},{5,69},{6,70},{7,71},{8,72},{9,... | collective-permute-start | bytes 393224 | tf_op jit(solution)/shard_map/ppermute | solution.py:393
  184.1 7.9 %collective-permute-start.11 = (bf16[512,128]{1,0:T(8,128)(2,1)}, bf16[512,128]{1,0:T(8,128)(2,1)S(1)}, u32[]{:S(2)}, u32[]{:S(2)}) collective-permute-start(bf16[512,128]{1,0:T(8,128)(2,1)} %get-tuple-element.40), channel_id=1, source_target_pairs={{0,32},{1,33},{2,34},{3,35},{4,36},{5,37},{6,38},{7,39},{8,40},{9,... | collective-permute-start | bytes 393224 | tf_op jit(solution)/shard_map/ppermute | solution.py:393
  187.1 5.0 %copy-start.9 = (bf16[512,128]{1,0:T(8,128)(2,1)}, bf16[512,128]{1,0:T(8,128)(2,1)S(1)}, u32[]{:S(2)}) copy-start(bf16[512,128]{1,0:T(8,128)(2,1)S(1)} %collective-permute-done.9.refs_1_) | copy-start | bytes 393220
  187.3 4.8 %copy-start.10 = (bf16[512,128]{1,0:T(8,128)(2,1)}, bf16[512,128]{1,0:T(8,128)(2,1)S(1)}, u32[]{:S(2)}) copy-start(bf16[512,128]{1,0:T(8,128)(2,1)S(1)} %collective-permute-done.10.refs_2_) | copy-start | bytes 393220
  192.0 0.7 copy-start.11
where the time goes:
time: 198 us; the launch traced here: 195 us
  waiting for transfers between devices  81 us (41%)
  Pallas kernels  64.7 us (33%)
  starting transfers between devices  42.7 us (22%)
  local copies, waits for them, and re-layouts  5.52 us (3%)
    all_to_all x4, waiting for transfers between devices, swap(): return lax.all_to_all(x, 'seq', 0, 0, tiled=True, axis_index_groups=NEAR)  26.3 us
    ppermute x9, starting transfers between devices, hop(): lax.ppermute(x, 'seq', [(s, (s + PEERS * o) % count) for s in range(count)])  23.9 us
    pallas_call x2, Pallas kernels, attend(): call(attend_body, jax.ShapeDtypeStruct((PEERS, MSG_OUT, HEAD), bf16), [pl...  21.4 us
    ppermute x9, waiting for transfers between devices, hop(): lax.ppermute(x, 'seq', [(s, (s + PEERS * o) % count) for s in range(count)])  20 us
    ppermute x1, waiting for transfers between devices, routed(): halo = lax.ppermute(tails[0], 'seq', NEXT)  18.9 us
    all_to_all x4, starting transfers between devices, swap(): return lax.all_to_all(x, 'seq', 0, 0, tiled=True, axis_index_groups=NEAR)  17.9 us
    ppermute x1, waiting for transfers between devices, routed(): halo = lax.ppermute(tails[1], 'seq', NEXT)  11.3 us
    pallas_call x2, Pallas kernels, pack(): call(body, (jax.ShapeDtypeStruct(shape, bf16), jax.ShapeDtypeStruct((HOPS...  9.83 us
  transfers between devices with their start and end apart: 16, of which 9 were waited for; matrix products, arithmetic and copies ran while one was open for 0% of the time, Pallas kernels for 26%

commit v1 on v0

--- a/solution.py
+++ b/solution.py
@@ -17,6 +17,7 @@
 MSG = STR * PB
 SLOTS = PEERS * PB
 PLACES = PEERS * STR * UNIT
+GRANT = 16 << 20
 EXTRA = 16
 SIDE = 8
 MSG_OUT = MSG + SIDE
@@ -52,7 +53,7 @@
         body,
         out_shape=out_shape,
         scratch_shapes=list(scratch),
-        compiler_params=pltpu.CompilerParams(vmem_limit_bytes=56 << 20),
+        compiler_params=pltpu.CompilerParams(vmem_limit_bytes=GRANT),
         **kw,
     )
 
@@ -111,7 +112,7 @@
 
 
 SMEM = pl.BlockSpec(memory_space=pltpu.SMEM)
-HBM = pl.BlockSpec(memory_space=pl.ANY)
+HBM = pl.BlockSpec(memory_space=pltpu.HBM)
 
 
 def split_heads(spot, qk, values):
@@ -186,9 +187,9 @@
 
 
 def tail_of(x):
-    return pl.pallas_call(
+    return call(
         tail_body,
-        out_shape=jax.ShapeDtypeStruct((ROWS, 2 * HEAD), bf16),
+        jax.ShapeDtypeStruct((ROWS, 2 * HEAD), bf16),
         grid=(1,),
         in_specs=[pl.BlockSpec((PEERS, PB + UNIT, 2 * HEAD), lambda i: (0, 2, 0))],
         out_specs=pl.BlockSpec((ROWS, 2 * HEAD), lambda i: (0, 0)),

time: 198 us -> 185 us (0.934)
  Pallas kernels: 64.7 us -> 40.5 us
  waiting for transfers between devices: 81 us -> 94.4 us
    pallas_call x2, Pallas kernels: 8.06 us -> 3.25 us  [compact(): call(compact_body, (jax.ShapeDtypeStruct((STR * ROWS, 2 * HEAD), bf16), j...]
    ppermute x1, waiting for transfers between devices: 11.3 us -> 15.3 us  [routed(): halo = lax.ppermute(tails[1], 'seq', NEXT)]
    pallas_call x2, Pallas kernels: 9.43 us -> 5.35 us  [merge(): call(body, (jax.ShapeDtypeStruct((ROWS, HEAD), bf16),) * len(slots), [plt...]
    ppermute x1, waiting for transfers between devices: 18.9 us -> 22.9 us  [routed(): halo = lax.ppermute(tails[0], 'seq', NEXT)]
    pallas_call x2, Pallas kernels: 9.83 us -> 6.21 us  [pack(): call(body, (jax.ShapeDtypeStruct(shape, bf16), jax.ShapeDtypeStruct((HOPS...]
    pallas_call x2, Pallas kernels: 4.88 us -> 1.34 us  [tail_of(): call(tail_body, jax.ShapeDtypeStruct((ROWS, 2 * HEAD), bf16), grid=(1,),...]
    all_to_all x4, waiting for transfers between devices: 26.3 us -> 29.5 us  [swap(): return lax.all_to_all(x, 'seq', 0, 0, tiled=True, axis_index_groups=NEAR)]
    pallas_call x2, Pallas kernels: 21.4 us -> 18.6 us  [attend(): call(attend_body, jax.ShapeDtypeStruct((PEERS, MSG_OUT, HEAD), bf16), [pl...]
  transfers between devices with their start and end apart: 16 -> 16, of which waited for: 9 -> 9; matrix products, arithmetic and copies ran while one was open for 0% -> 0% of each run, Pallas kernels for 26% -> 17%
where the time goes in v1:
time: 185 us; the launch traced here: 182 us
  waiting for transfers between devices  94.4 us (51%)
  starting transfers between devices  43.3 us (23%)
  Pallas kernels  40.5 us (22%)
  local copies, waits for them, and re-layouts  3.64 us (2%)
    all_to_all x4, waiting for transfers between devices, swap(): return lax.all_to_all(x, 'seq', 0, 0, tiled=True, axis_index_groups=NEAR)  29.5 us
    ppermute x9, starting transfers between devices, hop(): lax.ppermute(x, 'seq', [(s, (s + PEERS * o) % count) for s in range(count)])  24.1 us
    ppermute x1, waiting for transfers between devices, routed(): halo = lax.ppermute(tails[0], 'seq', NEXT)  22.9 us
    ppermute x9, waiting for transfers between devices, hop(): lax.ppermute(x, 'seq', [(s, (s + PEERS * o) % count) for s in range(count)])  22.1 us
    pallas_call x2, Pallas kernels, attend(): call(attend_body, jax.ShapeDtypeStruct((PEERS, MSG_OUT, HEAD), bf16), [pl...  18.6 us
    all_to_all x4, starting transfers between devices, swap(): return lax.all_to_all(x, 'seq', 0, 0, tiled=True, axis_index_groups=NEAR)  17.9 us
    ppermute x1, waiting for transfers between devices, routed(): halo = lax.ppermute(tails[1], 'seq', NEXT)  15.3 us
    pallas_call x2, Pallas kernels, pack(): call(body, (jax.ShapeDtypeStruct(shape, bf16), jax.ShapeDtypeStruct((HOPS...  6.21 us
  transfers between devices with their start and end apart: 16, of which 9 were waited for; matrix products, arithmetic and copies ran while one was open for 0% of the time, Pallas kernels for 17%

profile of v1, /device:TPU:4, one launch (start us, length us, event | category | flops | bytes accessed | tf_op | source)
XLA Modules:
  0.0 181.9 jit_solution(5057198433537581296)
XLA Ops:
  0.0 0.0 copy-start.3
  0.0 0.1 pad_add_fusion.spot_ref
  0.1 0.0 copy-start.1
  0.1 1.2 copy-done.1
  1.3 0.0 copy-start.2
  1.3 1.2 copy-done.2
  2.5 0.9 split_heads.1
  3.4 3.3 %collective-permute-start = (bf16[512,256]{1,0:T(8,128)(2,1)S(1)}, bf16[512,256]{1,0:T(8,128)(2,1)S(1)}, u32[]{:S(2)}, u32[]{:S(2)}) collective-permute-start(bf16[512,256]{1,0:T(8,128)(2,1)S(1)} %get-tuple-element.24), channel_id=1, source_target_pairs={{0,32},{1,33},{2,34},{3,35},{4,36},{5,37},{6,38},{7,39},{8,40},{9,... | collective-permute-start | bytes 786440 | tf_op jit(solution)/shard_map/ppermute | solution.py:394
  6.8 5.4 %collective-permute-start.1 = (bf16[512,256]{1,0:T(8,128)(2,1)S(1)}, bf16[512,256]{1,0:T(8,128)(2,1)S(1)}, u32[]{:S(2)}, u32[]{:S(2)}) collective-permute-start(bf16[512,256]{1,0:T(8,128)(2,1)S(1)} %get-tuple-element.25), channel_id=1, source_target_pairs={{0,64},{1,65},{2,66},{3,67},{4,68},{5,69},{6,70},{7,71},{8,72},{9,... | collective-permute-start | bytes 786440 | tf_op jit(solution)/shard_map/ppermute | solution.py:394
  12.2 2.7 %collective-permute-start.2 = (bf16[512,256]{1,0:T(8,128)(2,1)S(1)}, bf16[512,256]{1,0:T(8,128)(2,1)S(1)}, u32[]{:S(2)}, u32[]{:S(2)}) collective-permute-start(bf16[512,256]{1,0:T(8,128)(2,1)S(1)} %get-tuple-element.26), channel_id=1, source_target_pairs={{0,96},{1,97},{2,98},{3,99},{4,100},{5,101},{6,102},{7,103},{8,104... | collective-permute-start | bytes 786440 | tf_op jit(solution)/shard_map/ppermute | solution.py:394
  14.9 0.0 copy-done.3
  14.9 0.5 collective-permute-start.3
  15.4 4.6 %collective-permute-done.3.other_ref = s32[1,512]{1,0:T(1,128)S(1)} collective-permute-done((s32[1,512]{1,0:T(1,128)S(1)}, s32[1,512]{1,0:T(1,128)S(1)}, u32[]{:S(2)}, u32[]{:S(2)}) %collective-permute-start.3) | collective-permute-done | bytes 2080 | tf_op jit(solution)/shard_map/ppermute | solution.py:407
  19.9 1.0 places.1.refs_4_
  20.9 0.1 collective-permute-start.6
  21.0 3.8 %collective-permute-start.5 = (bf16[16,256]{1,0:T(8,128)(2,1)S(1)}, bf16[16,256]{1,0:T(8,128)(2,1)S(1)}, u32[]{:S(2)}, u32[]{:S(2)}) collective-permute-start(bf16[16,256]{1,0:T(8,128)(2,1)S(1)} %places.1.refs_4_), channel_id=1, source_target_pairs={{0,64},{1,65},{2,66},{3,67},{4,68},{5,69},{6,70},{7,71},{8,72},{9,... | collective-permute-start | bytes 24584 | tf_op jit(solution)/shard_map/ppermute | solution.py:394
  24.8 11.6 %collective-permute-done.6.refs_7_ = bf16[16,256]{1,0:T(8,128)(2,1)S(1)} collective-permute-done((bf16[16,256]{1,0:T(8,128)(2,1)S(1)}, bf16[16,256]{1,0:T(8,128)(2,1)S(1)}, u32[]{:S(2)}, u32[]{:S(2)}) %collective-permute-start.6) | collective-permute-done | bytes 8224 | tf_op jit(solution)/shard_map/ppermute | solution.py:394
  36.4 1.5 collective-permute-start.4
  37.9 0.0 collective-permute-done.5.refs_6_
  37.9 4.2 %collective-permute-done.4.refs_5_ = bf16[16,256]{1,0:T(8,128)(2,1)S(1)} collective-permute-done((bf16[16,256]{1,0:T(8,128)(2,1)S(1)}, bf16[16,256]{1,0:T(8,128)(2,1)S(1)}, u32[]{:S(2)}, u32[]{:S(2)}) %collective-permute-start.4) | collective-permute-done | bytes 8224 | tf_op jit(solution)/shard_map/ppermute | solution.py:394
  42.2 0.0 collective-permute-done.refs_1_
  42.2 0.0 collective-permute-done.1.refs_2_
  42.2 0.0 collective-permute-done.2.refs_3_
  42.2 3.7 %pack.3 = (bf16[32,96,256]{2,1,0:T(8,128)(2,1)}, s32[4,512]{1,0:T(4,128)S(1)}) custom-call(bf16[512,256]{1,0:T(8,128)(2,1)S(1)} %get-tuple-element.23.refs_0_, bf16[512,256]{1,0:T(8,128)(2,1)S(1)} %collective-permute-done.refs_1_, bf16[512,256]{1,0:T(8,128)(2,1)S(1)} %collective-permute-done.1.refs_2_, bf16[512,256]{1,0:T(8,128)(2,1)S(1)} %collective-permute-done.2.refs_3_, ...), custom_call_target="tpu_custom_call" | custom-call | tf_op jit(solution)/shard_map/pack/pallas_call | solution.py:172
  45.9 5.5 %all-to-all-start.2 = ((bf16[32,96,256]{2,1,0:T(8,128)(2,1)}), bf16[32,96,256]{2,1,0:T(8,128)(2,1)S(1)}, u32[]{:S(2)}, u32[]{:S(2)}) async-start(bf16[32,96,256]{2,1,0:T(8,128)(2,1)} %get-tuple-element.32), calls=%async_computation.2 | async-start | bytes 3145728 | tf_op jit(solution)/shard_map/all_to_all | solution.py:398
  51.4 2.5 %pack.2 = (bf16[32,96,256]{2,1,0:T(8,128)(2,1)S(1)}, s32[4,512]{1,0:T(4,128)S(1)}) custom-call(bf16[512,256]{1,0:T(8,128)(2,1)S(1)} %get-tuple-element.23.refs_0_, bf16[512,256]{1,0:T(8,128)(2,1)S(1)} %collective-permute-done.refs_1_, bf16[512,256]{1,0:T(8,128)(2,1)S(1)} %collective-permute-done.1.refs_2_, ...), custom_call_target="tpu_custom_call" | custom-call | tf_op jit(solution)/shard_map/pack/pallas_call | solution.py:172
  53.9 0.0 copy-start
  53.9 1.2 copy-done
  55.1 17.9 %all-to-all-done.2.x_ref = bf16[32,96,256]{2,1,0:T(8,128)(2,1)S(1)} async-done(((bf16[32,96,256]{2,1,0:T(8,128)(2,1)}), bf16[32,96,256]{2,1,0:T(8,128)(2,1)S(1)}, u32[]{:S(2)}, u32[]{:S(2)}) %all-to-all-start.2) | async-done | bytes 1572896 | tf_op jit(solution)/shard_map/all_to_all | solution.py:398
  73.0 4.3 %all-to-all-start = ((bf16[32,96,256]{2,1,0:T(8,128)(2,1)}), bf16[32,96,256]{2,1,0:T(8,128)(2,1)S(1)}, u32[]{:S(2)}, u32[]{:S(2)}) async-start(bf16[32,96,256]{2,1,0:T(8,128)(2,1)} %copy-done), calls=%async_computation | async-start | bytes 3145728 | tf_op jit(solution)/shard_map/all_to_all | solution.py:398
  77.3 0.7 tail.3.tail_ref
  78.0 0.5 collective-permute-start.8
  78.5 1.6 compact.3
  80.2 22.9 %collective-permute-done.8.halo_ref = bf16[512,256]{1,0:T(8,128)(2,1)S(1)} collective-permute-done((bf16[512,256]{1,0:T(8,128)(2,1)S(1)}, bf16[512,256]{1,0:T(8,128)(2,1)S(1)}, u32[]{:S(2)}, u32[]{:S(2)}) %collective-permute-start.8) | collective-permute-done | bytes 262176 | tf_op jit(solution)/shard_map/ppermute | solution.py:416
  103.0 9.3 %attend.3 = bf16[32,104,128]{2,1,0:T(8,128)(2,1)} custom-call(bf16[2048,256]{1,0:T(8,128)(2,1)S(1)} %get-tuple-element.33.x_ref, bf16[512,256]{1,0:T(8,128)(2,1)S(1)} %collective-permute-done.8.halo_ref, f32[768,128]{1,0:T(8,128)S(1)} %get-tuple-element.34.tcol_ref), custom_call_target="tpu_custom_call" | custom-call | tf_op jit(solution)/shard_map/attend/pallas_call | solution.py:291
  112.3 0.0 all-to-all-done.x_ref
  112.3 3.9 %all-to-all-start.3 = ((bf16[32,104,128]{2,1,0:T(8,128)(2,1)}), bf16[32,104,128]{2,1,0:T(8,128)(2,1)S(1)}, u32[]{:S(2)}, u32[]{:S(2)}) async-start(bf16[32,104,128]{2,1,0:T(8,128)(2,1)} %attend.3), calls=%async_computation.3 | async-start | bytes 1703936 | tf_op jit(solution)/shard_map/all_to_all | solution.py:398
  116.3 0.7 tail.2.tail_ref
  116.9 0.2 collective-permute-start.7
  117.2 1.6 compact.2
  118.8 15.3 %collective-permute-done.7.halo_ref = bf16[512,256]{1,0:T(8,128)(2,1)S(1)} collective-permute-done((bf16[512,256]{1,0:T(8,128)(2,1)S(1)}, bf16[512,256]{1,0:T(8,128)(2,1)S(1)}, u32[]{:S(2)}, u32[]{:S(2)}) %collective-permute-start.7) | collective-permute-done | bytes 262176 | tf_op jit(solution)/shard_map/ppermute | solution.py:420
  134.1 9.3 %attend.2 = bf16[32,104,128]{2,1,0:T(8,128)(2,1)} custom-call(bf16[2048,256]{1,0:T(8,128)(2,1)S(1)} %get-tuple-element.29.x_ref, bf16[512,256]{1,0:T(8,128)(2,1)S(1)} %collective-permute-done.7.halo_ref, f32[768,128]{1,0:T(8,128)S(1)} %get-tuple-element.30.tcol_ref), custom_call_target="tpu_custom_call" | custom-call | tf_op jit(solution)/shard_map/attend/pallas_call | solution.py:291
  143.4 0.0 all-to-all-done.3.x_ref
  143.4 4.1 %all-to-all-start.1 = ((bf16[32,104,128]{2,1,0:T(8,128)(2,1)}), bf16[32,104,128]{2,1,0:T(8,128)(2,1)S(1)}, u32[]{:S(2)}, u32[]{:S(2)}) async-start(bf16[32,104,128]{2,1,0:T(8,128)(2,1)} %attend.2), calls=%async_computation.1 | async-start | bytes 1703936 | tf_op jit(solution)/shard_map/all_to_all | solution.py:398
  147.6 2.5 %unpack.1 = (bf16[4,512,128]{2,1,0:T(8,128)(2,1)S(1)}, f32[512,128]{1,0:T(8,128)S(1)}) custom-call(s32[4,512]{1,0:T(4,128)S(1)} %get-tuple-element.31.pos_ref, bf16[32,104,128]{2,1,0:T(8,128)(2,1)S(1)} %all-to-all-done.3.x_ref), custom_call_target="tpu_custom_call" | custom-call | tf_op jit(solution)/shard_map/unpack/pallas_call | solution.py:344
  150.0 11.6 %all-to-all-done.1.x_ref = bf16[32,104,128]{2,1,0:T(8,128)(2,1)S(1)} async-done(((bf16[32,104,128]{2,1,0:T(8,128)(2,1)}), bf16[32,104,128]{2,1,0:T(8,128)(2,1)S(1)}, u32[]{:S(2)}, u32[]{:S(2)}) %all-to-all-start.1) | async-done | bytes 852000 | tf_op jit(solution)/shard_map/all_to_all | solution.py:398
  161.6 2.7 %merge.3 = (bf16[512,128]{1,0:T(8,128)(2,1)S(1)}, bf16[512,128]{1,0:T(8,128)(2,1)S(1)}) custom-call(s32[4,512]{1,0:T(4,128)S(1)} %get-tuple-element.27.pos_ref, bf16[32,104,128]{2,1,0:T(8,128)(2,1)S(1)} %all-to-all-done.1.x_ref, bf16[4,512,128]{2,1,0:T(8,128)(2,1)S(1)} %get-tuple-element.35.other_ref, f32[512,128]{1,0:T(8,128)S(1)} %get-tuple-element.36.other_lse_ref), custom_call_target="tpu_custom_call" | custom-call | tf_op jit(solution)/shard_map/merge/pallas_call | solution.py:362
  164.3 2.4 %collective-permute-start.9 = (bf16[512,128]{1,0:T(8,128)(2,1)S(1)}, bf16[512,128]{1,0:T(8,128)(2,1)S(1)}, u32[]{:S(2)}, u32[]{:S(2)}) collective-permute-start(bf16[512,128]{1,0:T(8,128)(2,1)S(1)} %get-tuple-element.38), channel_id=1, source_target_pairs={{0,96},{1,97},{2,98},{3,99},{4,100},{5,101},{6,102},{7,103},{8,104... | collective-permute-start | bytes 393224 | tf_op jit(solution)/shard_map/ppermute | solution.py:394
  166.7 2.0 %collective-permute-start.10 = (bf16[512,128]{1,0:T(8,128)(2,1)S(1)}, bf16[512,128]{1,0:T(8,128)(2,1)S(1)}, u32[]{:S(2)}, u32[]{:S(2)}) collective-permute-start(bf16[512,128]{1,0:T(8,128)(2,1)S(1)} %get-tuple-element.39), channel_id=1, source_target_pairs={{0,64},{1,65},{2,66},{3,67},{4,68},{5,69},{6,70},{7,71},{8,72},{9,... | collective-permute-start | bytes 393224 | tf_op jit(solution)/shard_map/ppermute | solution.py:394
  168.7 2.7 %merge.2 = (bf16[512,128]{1,0:T(8,128)(2,1)S(1)}, bf16[512,128]{1,0:T(8,128)(2,1)S(1)}) custom-call(s32[4,512]{1,0:T(4,128)S(1)} %get-tuple-element.27.pos_ref, bf16[32,104,128]{2,1,0:T(8,128)(2,1)S(1)} %all-to-all-done.1.x_ref, bf16[4,512,128]{2,1,0:T(8,128)(2,1)S(1)} %get-tuple-element.35.other_ref, f32[512,128]{1,0:T(8,128)S(1)} %get-tuple-element.36.other_lse_ref), custom_call_target="tpu_custom_call" | custom-call | tf_op jit(solution)/shard_map/merge/pallas_call | solution.py:362
  171.3 2.9 %collective-permute-start.11 = (bf16[512,128]{1,0:T(8,128)(2,1)S(1)}, bf16[512,128]{1,0:T(8,128)(2,1)S(1)}, u32[]{:S(2)}, u32[]{:S(2)}) collective-permute-start(bf16[512,128]{1,0:T(8,128)(2,1)S(1)} %get-tuple-element.40), channel_id=1, source_target_pairs={{0,32},{1,33},{2,34},{3,35},{4,36},{5,37},{6,38},{7,39},{8,40},{9,... | collective-permute-start | bytes 393224 | tf_op jit(solution)/shard_map/ppermute | solution.py:394
  174.2 0.0 collective-permute-done.9.refs_1_
  174.2 2.0 %collective-permute-done.10.refs_2_ = bf16[512,128]{1,0:T(8,128)(2,1)S(1)} collective-permute-done((bf16[512,128]{1,0:T(8,128)(2,1)S(1)}, bf16[512,128]{1,0:T(8,128)(2,1)S(1)}, u32[]{:S(2)}, u32[]{:S(2)}) %collective-permute-start.10) | collective-permute-done | bytes 131104 | tf_op jit(solution)/shard_map/ppermute | solution.py:394
  176.2 4.3 %collective-permute-done.11.refs_3_ = bf16[512,128]{1,0:T(8,128)(2,1)S(1)} collective-permute-done((bf16[512,128]{1,0:T(8,128)(2,1)S(1)}, bf16[512,128]{1,0:T(8,128)(2,1)S(1)}, u32[]{:S(2)}, u32[]{:S(2)}) %collective-permute-start.11) | collective-permute-done | bytes 131104 | tf_op jit(solution)/shard_map/ppermute | solution.py:394
  180.5 1.4 join_heads.1
Async XLA Ops:
  0.0 14.9 %copy-start.3 = (s32[1,512]{1,0:T(1,128)S(1)}, s32[1,512]{1,0:T(1,128)}, u32[]{:S(2)}) copy-start(s32[1,512]{1,0:T(1,128)} %own_ref.1) | copy-start | bytes 6148
  0.1 1.2 copy-start.1
  1.3 1.2 copy-start.2
  3.4 38.7 %collective-permute-start = (bf16[512,256]{1,0:T(8,128)(2,1)S(1)}, bf16[512,256]{1,0:T(8,128)(2,1)S(1)}, u32[]{:S(2)}, u32[]{:S(2)}) collective-permute-start(bf16[512,256]{1,0:T(8,128)(2,1)S(1)} %get-tuple-element.24), channel_id=1, source_target_pairs={{0,32},{1,33},{2,34},{3,35},{4,36},{5,37},{6,38},{7,39},{8,40},{9,... | collective-permute-start | bytes 786440 | tf_op jit(solution)/shard_map/ppermute | solution.py:394
  6.8 35.4 %collective-permute-start.1 = (bf16[512,256]{1,0:T(8,128)(2,1)S(1)}, bf16[512,256]{1,0:T(8,128)(2,1)S(1)}, u32[]{:S(2)}, u32[]{:S(2)}) collective-permute-start(bf16[512,256]{1,0:T(8,128)(2,1)S(1)} %get-tuple-element.25), channel_id=1, source_target_pairs={{0,64},{1,65},{2,66},{3,67},{4,68},{5,69},{6,70},{7,71},{8,72},{9,... | collective-permute-start | bytes 786440 | tf_op jit(solution)/shard_map/ppermute | solution.py:394
  12.2 30.0 %collective-permute-start.2 = (bf16[512,256]{1,0:T(8,128)(2,1)S(1)}, bf16[512,256]{1,0:T(8,128)(2,1)S(1)}, u32[]{:S(2)}, u32[]{:S(2)}) collective-permute-start(bf16[512,256]{1,0:T(8,128)(2,1)S(1)} %get-tuple-element.26), channel_id=1, source_target_pairs={{0,96},{1,97},{2,98},{3,99},{4,100},{5,101},{6,102},{7,103},{8,104... | collective-permute-start | bytes 786440 | tf_op jit(solution)/shard_map/ppermute | solution.py:394
  14.9 5.1 %collective-permute-start.3 = (s32[1,512]{1,0:T(1,128)S(1)}, s32[1,512]{1,0:T(1,128)S(1)}, u32[]{:S(2)}, u32[]{:S(2)}) collective-permute-start(s32[1,512]{1,0:T(1,128)S(1)} %copy-done.3), channel_id=1, source_target_pairs={{0,128},{128,0},{1,129},{129,1},{2,130},{130,2},{3,131},{131,3},{4... | collective-permute-start | bytes 6152 | tf_op jit(solution)/shard_map/ppermute | solution.py:407
  20.9 15.5 %collective-permute-start.6 = (bf16[16,256]{1,0:T(8,128)(2,1)S(1)}, bf16[16,256]{1,0:T(8,128)(2,1)S(1)}, u32[]{:S(2)}, u32[]{:S(2)}) collective-permute-start(bf16[16,256]{1,0:T(8,128)(2,1)S(1)} %places.1.refs_4_), channel_id=1, source_target_pairs={{0,96},{1,97},{2,98},{3,99},{4,100},{5,101},{6,102},{7,103},{8,104... | collective-permute-start | bytes 24584 | tf_op jit(solution)/shard_map/ppermute | solution.py:394
  21.0 16.9 %collective-permute-start.5 = (bf16[16,256]{1,0:T(8,128)(2,1)S(1)}, bf16[16,256]{1,0:T(8,128)(2,1)S(1)}, u32[]{:S(2)}, u32[]{:S(2)}) collective-permute-start(bf16[16,256]{1,0:T(8,128)(2,1)S(1)} %places.1.refs_4_), channel_id=1, source_target_pairs={{0,64},{1,65},{2,66},{3,67},{4,68},{5,69},{6,70},{7,71},{8,72},{9,... | collective-permute-start | bytes 24584 | tf_op jit(solution)/shard_map/ppermute | solution.py:394
  36.4 5.8 %collective-permute-start.4 = (bf16[16,256]{1,0:T(8,128)(2,1)S(1)}, bf16[16,256]{1,0:T(8,128)(2,1)S(1)}, u32[]{:S(2)}, u32[]{:S(2)}) collective-permute-start(bf16[16,256]{1,0:T(8,128)(2,1)S(1)} %places.1.refs_4_), channel_id=1, source_target_pairs={{0,32},{1,33},{2,34},{3,35},{4,36},{5,37},{6,38},{7,39},{8,40},{9,... | collective-permute-start | bytes 24584 | tf_op jit(solution)/shard_map/ppermute | solution.py:394
  45.9 27.2 %all-to-all-start.2 = ((bf16[32,96,256]{2,1,0:T(8,128)(2,1)}), bf16[32,96,256]{2,1,0:T(8,128)(2,1)S(1)}, u32[]{:S(2)}, u32[]{:S(2)}) async-start(bf16[32,96,256]{2,1,0:T(8,128)(2,1)} %get-tuple-element.32), calls=%async_computation.2 | async-start | bytes 3145728 | tf_op jit(solution)/shard_map/all_to_all | solution.py:398
  53.9 1.2 copy-start
  73.0 39.3 %all-to-all-start = ((bf16[32,96,256]{2,1,0:T(8,128)(2,1)}), bf16[32,96,256]{2,1,0:T(8,128)(2,1)S(1)}, u32[]{:S(2)}, u32[]{:S(2)}) async-start(bf16[32,96,256]{2,1,0:T(8,128)(2,1)} %copy-done), calls=%async_computation | async-start | bytes 3145728 | tf_op jit(solution)/shard_map/all_to_all | solution.py:398
  78.0 25.0 %collective-permute-start.8 = (bf16[512,256]{1,0:T(8,128)(2,1)S(1)}, bf16[512,256]{1,0:T(8,128)(2,1)S(1)}, u32[]{:S(2)}, u32[]{:S(2)}) collective-permute-start(bf16[512,256]{1,0:T(8,128)(2,1)S(1)} %tail.3.tail_ref), channel_id=1, source_target_pairs={{0,1},{1,2},{2,3},{3,4},{4,5},{5,6},{6,7},{7,8},{8,9},{9,10},{10,1... | collective-permute-start | bytes 786440 | tf_op jit(solution)/shard_map/ppermute | solution.py:416
  112.3 31.1 %all-to-all-start.3 = ((bf16[32,104,128]{2,1,0:T(8,128)(2,1)}), bf16[32,104,128]{2,1,0:T(8,128)(2,1)S(1)}, u32[]{:S(2)}, u32[]{:S(2)}) async-start(bf16[32,104,128]{2,1,0:T(8,128)(2,1)} %attend.3), calls=%async_computation.3 | async-start | bytes 1703936 | tf_op jit(solution)/shard_map/all_to_all | solution.py:398
  116.9 17.2 %collective-permute-start.7 = (bf16[512,256]{1,0:T(8,128)(2,1)S(1)}, bf16[512,256]{1,0:T(8,128)(2,1)S(1)}, u32[]{:S(2)}, u32[]{:S(2)}) collective-permute-start(bf16[512,256]{1,0:T(8,128)(2,1)S(1)} %tail.2.tail_ref), channel_id=1, source_target_pairs={{0,1},{1,2},{2,3},{3,4},{4,5},{5,6},{6,7},{7,8},{8,9},{9,10},{10,1... | collective-permute-start | bytes 786440 | tf_op jit(solution)/shard_map/ppermute | solution.py:420
  143.4 18.2 %all-to-all-start.1 = ((bf16[32,104,128]{2,1,0:T(8,128)(2,1)}), bf16[32,104,128]{2,1,0:T(8,128)(2,1)S(1)}, u32[]{:S(2)}, u32[]{:S(2)}) async-start(bf16[32,104,128]{2,1,0:T(8,128)(2,1)} %attend.2), calls=%async_computation.1 | async-start | bytes 1703936 | tf_op jit(solution)/shard_map/all_to_all | solution.py:398
  164.3 10.0 %collective-permute-start.9 = (bf16[512,128]{1,0:T(8,128)(2,1)S(1)}, bf16[512,128]{1,0:T(8,128)(2,1)S(1)}, u32[]{:S(2)}, u32[]{:S(2)}) collective-permute-start(bf16[512,128]{1,0:T(8,128)(2,1)S(1)} %get-tuple-element.38), channel_id=1, source_target_pairs={{0,96},{1,97},{2,98},{3,99},{4,100},{5,101},{6,102},{7,103},{8,104... | collective-permute-start | bytes 393224 | tf_op jit(solution)/shard_map/ppermute | solution.py:394
  166.7 9.6 %collective-permute-start.10 = (bf16[512,128]{1,0:T(8,128)(2,1)S(1)}, bf16[512,128]{1,0:T(8,128)(2,1)S(1)}, u32[]{:S(2)}, u32[]{:S(2)}) collective-permute-start(bf16[512,128]{1,0:T(8,128)(2,1)S(1)} %get-tuple-element.39), channel_id=1, source_target_pairs={{0,64},{1,65},{2,66},{3,67},{4,68},{5,69},{6,70},{7,71},{8,72},{9,... | collective-permute-start | bytes 393224 | tf_op jit(solution)/shard_map/ppermute | solution.py:394
  171.3 9.2 %collective-permute-start.11 = (bf16[512,128]{1,0:T(8,128)(2,1)S(1)}, bf16[512,128]{1,0:T(8,128)(2,1)S(1)}, u32[]{:S(2)}, u32[]{:S(2)}) collective-permute-start(bf16[512,128]{1,0:T(8,128)(2,1)S(1)} %get-tuple-element.40), channel_id=1, source_target_pairs={{0,32},{1,33},{2,34},{3,35},{4,36},{5,37},{6,38},{7,39},{8,40},{9,... | collective-permute-start | bytes 393224 | tf_op jit(solution)/shard_map/ppermute | solution.py:394

commit v2 on v1

--- a/solution.py
+++ b/solution.py
@@ -17,7 +17,6 @@
 MSG = STR * PB
 SLOTS = PEERS * PB
 PLACES = PEERS * STR * UNIT
-GRANT = 16 << 20
 EXTRA = 16
 SIDE = 8
 MSG_OUT = MSG + SIDE
@@ -48,12 +47,12 @@
     return jnp.where(mask, 1.0, 0.0).astype(bf16)
 
 
-def call(body, out_shape, scratch=(), **kw):
+def call(body, out_shape, scratch=(), grant=16 << 20, **kw):
     return pl.pallas_call(
         body,
         out_shape=out_shape,
         scratch_shapes=list(scratch),
-        compiler_params=pltpu.CompilerParams(vmem_limit_bytes=GRANT),
+        compiler_params=pltpu.CompilerParams(vmem_limit_bytes=grant),
         **kw,
     )
 
@@ -95,34 +94,33 @@
     return pl.ds(pl.multiple_of(spot * HEAD, HEAD), HEAD)
 
 
-def split_body(spot_ref, qk_ref, v_ref, *refs):
-    outs, sems = refs[:HOPS], refs[HOPS]
-    copies = []
-    for o in range(HOPS):
-        head = spot_ref[0] * HOPS + ((spot_ref[1] + o) & (HOPS - 1))
-        for n, ref in enumerate((qk_ref, v_ref)):
-            copies.append(
-                pltpu.make_async_copy(
-                    ref.at[:, lanes_of(head)],
-                    outs[o].at[:, n * HEAD : (n + 1) * HEAD],
-                    sems.at[o * 2 + n],
+def split_heads(spot, qk, values, slots):
+    def body(spot_ref, qk_ref, v_ref, *refs):
+        copies = []
+        for i, o in enumerate(slots):
+            head = spot_ref[0] * HOPS + ((spot_ref[1] + o) & (HOPS - 1))
+            for n, ref in enumerate((qk_ref, v_ref)):
+                copies.append(
+                    pltpu.make_async_copy(
+                        ref.at[:, lanes_of(head)],
+                        refs[i].at[:, n * HEAD : (n + 1) * HEAD],
+                        refs[-1].at[i * 2 + n],
+                    )
                 )
-            )
-    copy_all(copies)
-
-
-SMEM = pl.BlockSpec(memory_space=pltpu.SMEM)
-HBM = pl.BlockSpec(memory_space=pltpu.HBM)
-
-
-def split_heads(spot, qk, values):
-    return call(
-        split_body,
-        (jax.ShapeDtypeStruct((ROWS, 2 * HEAD), bf16),) * HOPS,
-        [pltpu.SemaphoreType.DMA((2 * HOPS,))],
+        copy_all(copies)
+
+    return call(
+        body,
+        (jax.ShapeDtypeStruct((ROWS, 2 * HEAD), bf16),) * len(slots),
+        [pltpu.SemaphoreType.DMA((2 * len(slots),))],
+        grant=56 << 20,
         in_specs=[SMEM, HBM, HBM],
         name="split_heads",
     )(spot, qk, values)
+
+
+SMEM = pl.BlockSpec(memory_space=pltpu.SMEM)
+HBM = pl.BlockSpec(memory_space=pltpu.HBM)
 
 
 def place_body(spot_ref, own_ref, other_ref, o_ref):
@@ -386,7 +384,6 @@
 
 NEAR = [[PEERS * j + p for p in range(PEERS)] for j in range(HOPS)]
 NEXT = [(PEERS * j + p, PEERS * j + (p + 1) % PEERS) for j in range(HOPS) for p in range(PEERS)]
-ORDER = (2, 1, 3)
 
 
 def hop(x, o):
@@ -405,9 +402,13 @@
 def routed(qk, values, dest_dev):
     spot = jnp.stack([lax.axis_index("round"), lax.axis_index("seq") // PEERS]).astype(i32)
     other = lax.ppermute(dest_dev, "round", [(0, 1), (1, 0)])
-    mine = list(split_heads(spot, qk, values))
-    for o in ORDER:
+    mine = {}
+    (mine[2],) = split_heads(spot, qk, values, (2,))
+    mine[2] = hop(mine[2], 2)
+    mine[1], mine[3], mine[0] = split_heads(spot, qk, values, (1, 3, 0))
+    for o in (1, 3):
         mine[o] = hop(mine[o], o)
+    mine = [mine[o] for o in range(HOPS)]
     here = places(spot, dest_dev, other)
     spots = [here] + [hop(here, o) for o in range(1, HOPS)]
     sent, pos = zip(*[pack(mine, spots, r) for r in range(2)])

time: 185 us -> 184 us (level)
  Pallas kernels: 40.5 us -> 44.8 us
  starting transfers between devices: 43.3 us -> 40.6 us
    pallas_call x1 -> x2, Pallas kernels: 0.91 us -> 5.17 us  [split_heads(): call(body, (jax.ShapeDtypeStruct((ROWS, 2 * HEAD), bf16),) * len(slots),...]
    ppermute x9, starting transfers between devices: 24.1 us -> 21.3 us  [hop(): lax.ppermute(x, 'seq', [(s, (s + PEERS * o) % count) for s in range(count)])]
  transfers between devices with their start and end apart: 16 -> 16, of which waited for: 9 -> 10; matrix products, arithmetic and copies ran while one was open for 0% -> 0% of each run, Pallas kernels for 17% -> 19%
where the time goes in v2:
time: 184 us; the launch traced here: 182 us
  waiting for transfers between devices  93.2 us (51%)
  Pallas kernels  44.8 us (24%)
  starting transfers between devices  40.6 us (22%)
  local copies, waits for them, and re-layouts  2.14 us (1%)
    all_to_all x4, waiting for transfers between devices, swap(): return lax.all_to_all(x, 'seq', 0, 0, tiled=True, axis_index_groups=NEAR)  29.5 us
    ppermute x1, waiting for transfers between devices, routed(): halo = lax.ppermute(tails[0], 'seq', NEXT)  22.9 us
    ppermute x9, starting transfers between devices, hop(): lax.ppermute(x, 'seq', [(s, (s + PEERS * o) % count) for s in range(count)])  21.3 us
    ppermute x9, waiting for transfers between devices, hop(): lax.ppermute(x, 'seq', [(s, (s + PEERS * o) % count) for s in range(count)])  20.9 us
    pallas_call x2, Pallas kernels, attend(): call(attend_body, jax.ShapeDtypeStruct((PEERS, MSG_OUT, HEAD), bf16), [pl...  18.6 us
    all_to_all x4, starting transfers between devices, swap(): return lax.all_to_all(x, 'seq', 0, 0, tiled=True, axis_index_groups=NEAR)  18 us
    ppermute x1, waiting for transfers between devices, routed(): halo = lax.ppermute(tails[1], 'seq', NEXT)  15.3 us
    pallas_call x2, Pallas kernels, pack(): call(body, (jax.ShapeDtypeStruct(shape, bf16), jax.ShapeDtypeStruct((HOPS...  6.2 us
  transfers between devices with their start and end apart: 16, of which 10 were waited for; matrix products, arithmetic and copies ran while one was open for 0% of the time, Pallas kernels for 19%

profile of v2, /device:TPU:4, one launch (start us, length us, event | category | flops | bytes accessed | tf_op | source)
XLA Modules:
  0.0 181.5 jit_solution(15606488641057881190)
XLA Ops:
  0.0 0.6 pad_add_fusion.spot_ref
  0.6 2.4 %split_heads.3 = bf16[512,256]{1,0:T(8,128)(2,1)} custom-call(s32[2]{0:T(128)} %pad_add_fusion.spot_ref, bf16[512,1024]{1,0:T(8,128)(2,1)} %qk_ref.3, bf16[512,1024]{1,0:T(8,128)(2,1)} %v_ref.3), custom_call_target="tpu_custom_call" | custom-call | tf_op jit(solution)/shard_map/split_heads/pallas_call | solution.py:112
  3.0 0.0 copy-start.4
  3.0 0.0 copy-start.3
  3.0 7.3 %collective-permute-start.1 = (bf16[512,256]{1,0:T(8,128)(2,1)}, bf16[512,256]{1,0:T(8,128)(2,1)S(1)}, u32[]{:S(2)}, u32[]{:S(2)}) collective-permute-start(bf16[512,256]{1,0:T(8,128)(2,1)} %split_heads.3), channel_id=1, source_target_pairs={{0,64},{1,65},{2,66},{3,67},{4,68},{5,69},{6,70},{7,71},{8,72},{9,... | collective-permute-start | bytes 786440 | tf_op jit(solution)/shard_map/ppermute | solution.py:391
  10.3 2.8 %split_heads.2 = (bf16[512,256]{1,0:T(8,128)(2,1)}, bf16[512,256]{1,0:T(8,128)(2,1)}, bf16[512,256]{1,0:T(8,128)(2,1)}) custom-call(s32[2]{0:T(128)} %pad_add_fusion.spot_ref, bf16[512,1024]{1,0:T(8,128)(2,1)} %qk_ref.3, bf16[512,1024]{1,0:T(8,128)(2,1)} %v_ref.3), custom_call_target="tpu_custom_call" | custom-call | tf_op jit(solution)/shard_map/split_heads/pallas_call | solution.py:112
  13.1 1.6 collective-permute-start
  14.6 2.7 %collective-permute-start.2 = (bf16[512,256]{1,0:T(8,128)(2,1)}, bf16[512,256]{1,0:T(8,128)(2,1)S(1)}, u32[]{:S(2)}, u32[]{:S(2)}) collective-permute-start(bf16[512,256]{1,0:T(8,128)(2,1)} %get-tuple-element.24), channel_id=1, source_target_pairs={{0,96},{1,97},{2,98},{3,99},{4,100},{5,101},{6,102},{7,103},{8,104... | collective-permute-start | bytes 786440 | tf_op jit(solution)/shard_map/ppermute | solution.py:391
  17.3 0.0 copy-done.4
  17.3 0.5 collective-permute-start.3
  17.8 4.6 %collective-permute-done.3.other_ref = s32[1,512]{1,0:T(1,128)S(1)} collective-permute-done((s32[1,512]{1,0:T(1,128)S(1)}, s32[1,512]{1,0:T(1,128)S(1)}, u32[]{:S(2)}, u32[]{:S(2)}) %collective-permute-start.3) | collective-permute-done | bytes 2080 | tf_op jit(solution)/shard_map/ppermute | solution.py:404
  22.4 0.0 copy-done.3
  22.4 1.0 places.1.refs_4_
  23.4 0.1 collective-permute-start.6
  23.5 3.8 %collective-permute-start.5 = (bf16[16,256]{1,0:T(8,128)(2,1)S(1)}, bf16[16,256]{1,0:T(8,128)(2,1)S(1)}, u32[]{:S(2)}, u32[]{:S(2)}) collective-permute-start(bf16[16,256]{1,0:T(8,128)(2,1)S(1)} %places.1.refs_4_), channel_id=1, source_target_pairs={{0,64},{1,65},{2,66},{3,67},{4,68},{5,69},{6,70},{7,71},{8,72},{9,... | collective-permute-start | bytes 24584 | tf_op jit(solution)/shard_map/ppermute | solution.py:391
  27.3 7.6 %collective-permute-done.6.refs_7_ = bf16[16,256]{1,0:T(8,128)(2,1)S(1)} collective-permute-done((bf16[16,256]{1,0:T(8,128)(2,1)S(1)}, bf16[16,256]{1,0:T(8,128)(2,1)S(1)}, u32[]{:S(2)}, u32[]{:S(2)}) %collective-permute-start.6) | collective-permute-done | bytes 8224 | tf_op jit(solution)/shard_map/ppermute | solution.py:391
  34.9 0.4 collective-permute-start.4
  35.4 0.0 collective-permute-done.5.refs_6_
  35.4 5.3 %collective-permute-done.4.refs_5_ = bf16[16,256]{1,0:T(8,128)(2,1)S(1)} collective-permute-done((bf16[16,256]{1,0:T(8,128)(2,1)S(1)}, bf16[16,256]{1,0:T(8,128)(2,1)S(1)}, u32[]{:S(2)}, u32[]{:S(2)}) %collective-permute-start.4) | collective-permute-done | bytes 8224 | tf_op jit(solution)/shard_map/ppermute | solution.py:391
  40.7 0.0 collective-permute-done.1.refs_2_
  40.7 0.0 collective-permute-done.refs_1_
  40.7 0.0 collective-permute-done.2.refs_3_
  40.7 0.0 copy-start.1
  40.7 0.9 copy-done.1
  41.7 3.7 %pack.3 = (bf16[32,96,256]{2,1,0:T(8,128)(2,1)}, s32[4,512]{1,0:T(4,128)S(1)}) custom-call(bf16[512,256]{1,0:T(8,128)(2,1)S(1)} %copy-done.1, bf16[512,256]{1,0:T(8,128)(2,1)S(1)} %collective-permute-done.refs_1_, bf16[512,256]{1,0:T(8,128)(2,1)S(1)} %collective-permute-done.1.refs_2_, bf16[512,256]{1,0:T(8,128)(2,1)S(1)} %collective-permute-done.2.refs_3_, ...), custom_call_target="tpu_custom_call" | custom-call | tf_op jit(solution)/shard_map/pack/pallas_call | solution.py:170
  45.3 0.0 copy-start.2
  45.3 5.6 %all-to-all-start.2 = ((bf16[32,96,256]{2,1,0:T(8,128)(2,1)}), bf16[32,96,256]{2,1,0:T(8,128)(2,1)S(1)}, u32[]{:S(2)}, u32[]{:S(2)}) async-start(bf16[32,96,256]{2,1,0:T(8,128)(2,1)} %get-tuple-element.30), calls=%async_computation.2 | async-start | bytes 3145728 | tf_op jit(solution)/shard_map/all_to_all | solution.py:395
  51.0 0.0 copy-done.2
  51.0 2.5 %pack.2 = (bf16[32,96,256]{2,1,0:T(8,128)(2,1)S(1)}, s32[4,512]{1,0:T(4,128)S(1)}) custom-call(bf16[512,256]{1,0:T(8,128)(2,1)S(1)} %copy-done.2, bf16[512,256]{1,0:T(8,128)(2,1)S(1)} %collective-permute-done.refs_1_, bf16[512,256]{1,0:T(8,128)(2,1)S(1)} %collective-permute-done.1.refs_2_, bf16[512,256]{1,0:T(8,128)(2,1)S(1)} %collective-permute-done.2.refs_3_, ...), custom_call_target="tpu_custom_call" | custom-call | tf_op jit(solution)/shard_map/pack/pallas_call | solution.py:170
  53.5 0.0 copy-start
  53.5 1.2 copy-done
  54.7 17.9 %all-to-all-done.2.x_ref = bf16[32,96,256]{2,1,0:T(8,128)(2,1)S(1)} async-done(((bf16[32,96,256]{2,1,0:T(8,128)(2,1)}), bf16[32,96,256]{2,1,0:T(8,128)(2,1)S(1)}, u32[]{:S(2)}, u32[]{:S(2)}) %all-to-all-start.2) | async-done | bytes 1572896 | tf_op jit(solution)/shard_map/all_to_all | solution.py:395
  72.6 4.3 %all-to-all-start = ((bf16[32,96,256]{2,1,0:T(8,128)(2,1)}), bf16[32,96,256]{2,1,0:T(8,128)(2,1)S(1)}, u32[]{:S(2)}, u32[]{:S(2)}) async-start(bf16[32,96,256]{2,1,0:T(8,128)(2,1)} %copy-done), calls=%async_computation | async-start | bytes 3145728 | tf_op jit(solution)/shard_map/all_to_all | solution.py:395
  76.9 0.7 tail.3.tail_ref
  77.6 0.5 collective-permute-start.8
  78.1 1.6 compact.3
  79.8 22.9 %collective-permute-done.8.halo_ref = bf16[512,256]{1,0:T(8,128)(2,1)S(1)} collective-permute-done((bf16[512,256]{1,0:T(8,128)(2,1)S(1)}, bf16[512,256]{1,0:T(8,128)(2,1)S(1)}, u32[]{:S(2)}, u32[]{:S(2)}) %collective-permute-start.8) | collective-permute-done | bytes 262176 | tf_op jit(solution)/shard_map/ppermute | solution.py:417
  102.6 9.3 %attend.3 = bf16[32,104,128]{2,1,0:T(8,128)(2,1)} custom-call(bf16[2048,256]{1,0:T(8,128)(2,1)S(1)} %get-tuple-element.31.x_ref, bf16[512,256]{1,0:T(8,128)(2,1)S(1)} %collective-permute-done.8.halo_ref, f32[768,128]{1,0:T(8,128)S(1)} %get-tuple-element.32.tcol_ref), custom_call_target="tpu_custom_call" | custom-call | tf_op jit(solution)/shard_map/attend/pallas_call | solution.py:289
  112.0 0.0 all-to-all-done.x_ref
  112.0 3.9 %all-to-all-start.3 = ((bf16[32,104,128]{2,1,0:T(8,128)(2,1)}), bf16[32,104,128]{2,1,0:T(8,128)(2,1)S(1)}, u32[]{:S(2)}, u32[]{:S(2)}) async-start(bf16[32,104,128]{2,1,0:T(8,128)(2,1)} %attend.3), calls=%async_computation.3 | async-start | bytes 1703936 | tf_op jit(solution)/shard_map/all_to_all | solution.py:395
  115.9 0.7 tail.2.tail_ref
  116.6 0.2 collective-permute-start.7
  116.8 1.6 compact.2
  118.4 15.3 %collective-permute-done.7.halo_ref = bf16[512,256]{1,0:T(8,128)(2,1)S(1)} collective-permute-done((bf16[512,256]{1,0:T(8,128)(2,1)S(1)}, bf16[512,256]{1,0:T(8,128)(2,1)S(1)}, u32[]{:S(2)}, u32[]{:S(2)}) %collective-permute-start.7) | collective-permute-done | bytes 262176 | tf_op jit(solution)/shard_map/ppermute | solution.py:421
  133.8 9.3 %attend.2 = bf16[32,104,128]{2,1,0:T(8,128)(2,1)} custom-call(bf16[2048,256]{1,0:T(8,128)(2,1)S(1)} %get-tuple-element.27.x_ref, bf16[512,256]{1,0:T(8,128)(2,1)S(1)} %collective-permute-done.7.halo_ref, f32[768,128]{1,0:T(8,128)S(1)} %get-tuple-element.28.tcol_ref), custom_call_target="tpu_custom_call" | custom-call | tf_op jit(solution)/shard_map/attend/pallas_call | solution.py:289
  143.1 0.0 all-to-all-done.3.x_ref
  143.1 4.1 %all-to-all-start.1 = ((bf16[32,104,128]{2,1,0:T(8,128)(2,1)}), bf16[32,104,128]{2,1,0:T(8,128)(2,1)S(1)}, u32[]{:S(2)}, u32[]{:S(2)}) async-start(bf16[32,104,128]{2,1,0:T(8,128)(2,1)} %attend.2), calls=%async_computation.1 | async-start | bytes 1703936 | tf_op jit(solution)/shard_map/all_to_all | solution.py:395
  147.3 2.5 %unpack.1 = (bf16[4,512,128]{2,1,0:T(8,128)(2,1)S(1)}, f32[512,128]{1,0:T(8,128)S(1)}) custom-call(s32[4,512]{1,0:T(4,128)S(1)} %get-tuple-element.29.pos_ref, bf16[32,104,128]{2,1,0:T(8,128)(2,1)S(1)} %all-to-all-done.3.x_ref), custom_call_target="tpu_custom_call" | custom-call | tf_op jit(solution)/shard_map/unpack/pallas_call | solution.py:342
  149.7 11.6 %all-to-all-done.1.x_ref = bf16[32,104,128]{2,1,0:T(8,128)(2,1)S(1)} async-done(((bf16[32,104,128]{2,1,0:T(8,128)(2,1)}), bf16[32,104,128]{2,1,0:T(8,128)(2,1)S(1)}, u32[]{:S(2)}, u32[]{:S(2)}) %all-to-all-start.1) | async-done | bytes 852000 | tf_op jit(solution)/shard_map/all_to_all | solution.py:395
  161.3 2.7 %merge.3 = (bf16[512,128]{1,0:T(8,128)(2,1)S(1)}, bf16[512,128]{1,0:T(8,128)(2,1)S(1)}) custom-call(s32[4,512]{1,0:T(4,128)S(1)} %get-tuple-element.25.pos_ref, bf16[32,104,128]{2,1,0:T(8,128)(2,1)S(1)} %all-to-all-done.1.x_ref, bf16[4,512,128]{2,1,0:T(8,128)(2,1)S(1)} %get-tuple-element.33.other_ref, f32[512,128]{1,0:T(8,128)S(1)} %get-tuple-element.34.other_lse_ref), custom_call_target="tpu_custom_call" | custom-call | tf_op jit(solution)/shard_map/merge/pallas_call | solution.py:360
  164.0 2.6 %collective-permute-start.9 = (bf16[512,128]{1,0:T(8,128)(2,1)S(1)}, bf16[512,128]{1,0:T(8,128)(2,1)S(1)}, u32[]{:S(2)}, u32[]{:S(2)}) collective-permute-start(bf16[512,128]{1,0:T(8,128)(2,1)S(1)} %get-tuple-element.36), channel_id=1, source_target_pairs={{0,96},{1,97},{2,98},{3,99},{4,100},{5,101},{6,102},{7,103},{8,104... | collective-permute-start | bytes 393224 | tf_op jit(solution)/shard_map/ppermute | solution.py:391
  166.6 0.3 collective-permute-start.10
  166.8 2.7 %merge.2 = (bf16[512,128]{1,0:T(8,128)(2,1)S(1)}, bf16[512,128]{1,0:T(8,128)(2,1)S(1)}) custom-call(s32[4,512]{1,0:T(4,128)S(1)} %get-tuple-element.25.pos_ref, bf16[32,104,128]{2,1,0:T(8,128)(2,1)S(1)} %all-to-all-done.1.x_ref, bf16[4,512,128]{2,1,0:T(8,128)(2,1)S(1)} %get-tuple-element.33.other_ref, f32[512,128]{1,0:T(8,128)S(1)} %get-tuple-element.34.other_lse_ref), custom_call_target="tpu_custom_call" | custom-call | tf_op jit(solution)/shard_map/merge/pallas_call | solution.py:360
  169.5 2.7 %collective-permute-start.11 = (bf16[512,128]{1,0:T(8,128)(2,1)S(1)}, bf16[512,128]{1,0:T(8,128)(2,1)S(1)}, u32[]{:S(2)}, u32[]{:S(2)}) collective-permute-start(bf16[512,128]{1,0:T(8,128)(2,1)S(1)} %get-tuple-element.38), channel_id=1, source_target_pairs={{0,32},{1,33},{2,34},{3,35},{4,36},{5,37},{6,38},{7,39},{8,40},{9,... | collective-permute-start | bytes 393224 | tf_op jit(solution)/shard_map/ppermute | solution.py:391
  172.2 1.4 collective-permute-done.9.refs_1_
  173.6 5.8 %collective-permute-done.10.refs_2_ = bf16[512,128]{1,0:T(8,128)(2,1)S(1)} collective-permute-done((bf16[512,128]{1,0:T(8,128)(2,1)S(1)}, bf16[512,128]{1,0:T(8,128)(2,1)S(1)}, u32[]{:S(2)}, u32[]{:S(2)}) %collective-permute-start.10) | collective-permute-done | bytes 131104 | tf_op jit(solution)/shard_map/ppermute | solution.py:391
  179.4 0.7 collective-permute-done.11.refs_3_
  180.1 1.4 join_heads.1
Async XLA Ops:
  3.0 14.3 %copy-start.4 = (s32[1,512]{1,0:T(1,128)S(1)}, s32[1,512]{1,0:T(1,128)}, u32[]{:S(2)}) copy-start(s32[1,512]{1,0:T(1,128)} %own_ref.1) | copy-start | bytes 6148
  3.0 19.4 %copy-start.3 = (s32[2]{0:T(128)S(1)}, s32[2]{0:T(128)}, u32[]{:S(2)}) copy-start(s32[2]{0:T(128)} %pad_add_fusion.spot_ref) | copy-start | bytes 28
  3.0 37.7 %collective-permute-start.1 = (bf16[512,256]{1,0:T(8,128)(2,1)}, bf16[512,256]{1,0:T(8,128)(2,1)S(1)}, u32[]{:S(2)}, u32[]{:S(2)}) collective-permute-start(bf16[512,256]{1,0:T(8,128)(2,1)} %split_heads.3), channel_id=1, source_target_pairs={{0,64},{1,65},{2,66},{3,67},{4,68},{5,69},{6,70},{7,71},{8,72},{9,... | collective-permute-start | bytes 786440 | tf_op jit(solution)/shard_map/ppermute | solution.py:391
  13.1 27.6 %collective-permute-start = (bf16[512,256]{1,0:T(8,128)(2,1)}, bf16[512,256]{1,0:T(8,128)(2,1)S(1)}, u32[]{:S(2)}, u32[]{:S(2)}) collective-permute-start(bf16[512,256]{1,0:T(8,128)(2,1)} %get-tuple-element.23), channel_id=1, source_target_pairs={{0,32},{1,33},{2,34},{3,35},{4,36},{5,37},{6,38},{7,39},{8,40},{9,... | collective-permute-start | bytes 786440 | tf_op jit(solution)/shard_map/ppermute | solution.py:391
  14.6 26.1 %collective-permute-start.2 = (bf16[512,256]{1,0:T(8,128)(2,1)}, bf16[512,256]{1,0:T(8,128)(2,1)S(1)}, u32[]{:S(2)}, u32[]{:S(2)}) collective-permute-start(bf16[512,256]{1,0:T(8,128)(2,1)} %get-tuple-element.24), channel_id=1, source_target_pairs={{0,96},{1,97},{2,98},{3,99},{4,100},{5,101},{6,102},{7,103},{8,104... | collective-permute-start | bytes 786440 | tf_op jit(solution)/shard_map/ppermute | solution.py:391
  17.3 5.1 %collective-permute-start.3 = (s32[1,512]{1,0:T(1,128)S(1)}, s32[1,512]{1,0:T(1,128)S(1)}, u32[]{:S(2)}, u32[]{:S(2)}) collective-permute-start(s32[1,512]{1,0:T(1,128)S(1)} %copy-done.4), channel_id=1, source_target_pairs={{0,128},{128,0},{1,129},{129,1},{2,130},{130,2},{3,131},{131,3},{4... | collective-permute-start | bytes 6152 | tf_op jit(solution)/shard_map/ppermute | solution.py:404
  23.4 11.6 %collective-permute-start.6 = (bf16[16,256]{1,0:T(8,128)(2,1)S(1)}, bf16[16,256]{1,0:T(8,128)(2,1)S(1)}, u32[]{:S(2)}, u32[]{:S(2)}) collective-permute-start(bf16[16,256]{1,0:T(8,128)(2,1)S(1)} %places.1.refs_4_), channel_id=1, source_target_pairs={{0,96},{1,97},{2,98},{3,99},{4,100},{5,101},{6,102},{7,103},{8,104... | collective-permute-start | bytes 24584 | tf_op jit(solution)/shard_map/ppermute | solution.py:391
  23.5 11.9 %collective-permute-start.5 = (bf16[16,256]{1,0:T(8,128)(2,1)S(1)}, bf16[16,256]{1,0:T(8,128)(2,1)S(1)}, u32[]{:S(2)}, u32[]{:S(2)}) collective-permute-start(bf16[16,256]{1,0:T(8,128)(2,1)S(1)} %places.1.refs_4_), channel_id=1, source_target_pairs={{0,64},{1,65},{2,66},{3,67},{4,68},{5,69},{6,70},{7,71},{8,72},{9,... | collective-permute-start | bytes 24584 | tf_op jit(solution)/shard_map/ppermute | solution.py:391
  34.9 5.8 %collective-permute-start.4 = (bf16[16,256]{1,0:T(8,128)(2,1)S(1)}, bf16[16,256]{1,0:T(8,128)(2,1)S(1)}, u32[]{:S(2)}, u32[]{:S(2)}) collective-permute-start(bf16[16,256]{1,0:T(8,128)(2,1)S(1)} %places.1.refs_4_), channel_id=1, source_target_pairs={{0,32},{1,33},{2,34},{3,35},{4,36},{5,37},{6,38},{7,39},{8,40},{9,... | collective-permute-start | bytes 24584 | tf_op jit(solution)/shard_map/ppermute | solution.py:391
  40.7 1.0 copy-start.1
  45.3 5.6 %copy-start.2 = (bf16[512,256]{1,0:T(8,128)(2,1)S(1)}, bf16[512,256]{1,0:T(8,128)(2,1)}, u32[]{:S(2)}) copy-start(bf16[512,256]{1,0:T(8,128)(2,1)} %get-tuple-element.22.refs_0_) | copy-start | bytes 786436
  45.3 27.3 %all-to-all-start.2 = ((bf16[32,96,256]{2,1,0:T(8,128)(2,1)}), bf16[32,96,256]{2,1,0:T(8,128)(2,1)S(1)}, u32[]{:S(2)}, u32[]{:S(2)}) async-start(bf16[32,96,256]{2,1,0:T(8,128)(2,1)} %get-tuple-element.30), calls=%async_computation.2 | async-start | bytes 3145728 | tf_op jit(solution)/shard_map/all_to_all | solution.py:395
  53.5 1.2 copy-start
  72.6 39.4 %all-to-all-start = ((bf16[32,96,256]{2,1,0:T(8,128)(2,1)}), bf16[32,96,256]{2,1,0:T(8,128)(2,1)S(1)}, u32[]{:S(2)}, u32[]{:S(2)}) async-start(bf16[32,96,256]{2,1,0:T(8,128)(2,1)} %copy-done), calls=%async_computation | async-start | bytes 3145728 | tf_op jit(solution)/shard_map/all_to_all | solution.py:395
  77.6 25.0 %collective-permute-start.8 = (bf16[512,256]{1,0:T(8,128)(2,1)S(1)}, bf16[512,256]{1,0:T(8,128)(2,1)S(1)}, u32[]{:S(2)}, u32[]{:S(2)}) collective-permute-start(bf16[512,256]{1,0:T(8,128)(2,1)S(1)} %tail.3.tail_ref), channel_id=1, source_target_pairs={{0,1},{1,2},{2,3},{3,4},{4,5},{5,6},{6,7},{7,8},{8,9},{9,10},{10,1... | collective-permute-start | bytes 786440 | tf_op jit(solution)/shard_map/ppermute | solution.py:417
  112.0 31.1 %all-to-all-start.3 = ((bf16[32,104,128]{2,1,0:T(8,128)(2,1)}), bf16[32,104,128]{2,1,0:T(8,128)(2,1)S(1)}, u32[]{:S(2)}, u32[]{:S(2)}) async-start(bf16[32,104,128]{2,1,0:T(8,128)(2,1)} %attend.3), calls=%async_computation.3 | async-start | bytes 1703936 | tf_op jit(solution)/shard_map/all_to_all | solution.py:395
  116.6 17.2 %collective-permute-start.7 = (bf16[512,256]{1,0:T(8,128)(2,1)S(1)}, bf16[512,256]{1,0:T(8,128)(2,1)S(1)}, u32[]{:S(2)}, u32[]{:S(2)}) collective-permute-start(bf16[512,256]{1,0:T(8,128)(2,1)S(1)} %tail.2.tail_ref), channel_id=1, source_target_pairs={{0,1},{1,2},{2,3},{3,4},{4,5},{5,6},{6,7},{7,8},{8,9},{9,10},{10,1... | collective-permute-start | bytes 786440 | tf_op jit(solution)/shard_map/ppermute | solution.py:421
  143.1 18.2 %all-to-all-start.1 = ((bf16[32,104,128]{2,1,0:T(8,128)(2,1)}), bf16[32,104,128]{2,1,0:T(8,128)(2,1)S(1)}, u32[]{:S(2)}, u32[]{:S(2)}) async-start(bf16[32,104,128]{2,1,0:T(8,128)(2,1)} %attend.2), calls=%async_computation.1 | async-start | bytes 1703936 | tf_op jit(solution)/shard_map/all_to_all | solution.py:395
  164.0 9.6 %collective-permute-start.9 = (bf16[512,128]{1,0:T(8,128)(2,1)S(1)}, bf16[512,128]{1,0:T(8,128)(2,1)S(1)}, u32[]{:S(2)}, u32[]{:S(2)}) collective-permute-start(bf16[512,128]{1,0:T(8,128)(2,1)S(1)} %get-tuple-element.36), channel_id=1, source_target_pairs={{0,96},{1,97},{2,98},{3,99},{4,100},{5,101},{6,102},{7,103},{8,104... | collective-permute-start | bytes 393224 | tf_op jit(solution)/shard_map/ppermute | solution.py:391
  166.6 12.9 %collective-permute-start.10 = (bf16[512,128]{1,0:T(8,128)(2,1)S(1)}, bf16[512,128]{1,0:T(8,128)(2,1)S(1)}, u32[]{:S(2)}, u32[]{:S(2)}) collective-permute-start(bf16[512,128]{1,0:T(8,128)(2,1)S(1)} %get-tuple-element.37), channel_id=1, source_target_pairs={{0,64},{1,65},{2,66},{3,67},{4,68},{5,69},{6,70},{7,71},{8,72},{9,... | collective-permute-start | bytes 393224 | tf_op jit(solution)/shard_map/ppermute | solution.py:391
  169.5 10.6 %collective-permute-start.11 = (bf16[512,128]{1,0:T(8,128)(2,1)S(1)}, bf16[512,128]{1,0:T(8,128)(2,1)S(1)}, u32[]{:S(2)}, u32[]{:S(2)}) collective-permute-start(bf16[512,128]{1,0:T(8,128)(2,1)S(1)} %get-tuple-element.38), channel_id=1, source_target_pairs={{0,32},{1,33},{2,34},{3,35},{4,36},{5,37},{6,38},{7,39},{8,40},{9,... | collective-permute-start | bytes 393224 | tf_op jit(solution)/shard_map/ppermute | solution.py:391

commit v3 on v2

--- a/solution.py
+++ b/solution.py
@@ -94,7 +94,7 @@
     return pl.ds(pl.multiple_of(spot * HEAD, HEAD), HEAD)
 
 
-def split_heads(spot, qk, values, slots):
+def split_heads(spot, qk, values, slots, grant=56 << 20):
     def body(spot_ref, qk_ref, v_ref, *refs):
         copies = []
         for i, o in enumerate(slots):
@@ -113,7 +113,7 @@
         body,
         (jax.ShapeDtypeStruct((ROWS, 2 * HEAD), bf16),) * len(slots),
         [pltpu.SemaphoreType.DMA((2 * len(slots),))],
-        grant=56 << 20,
+        grant=grant,
         in_specs=[SMEM, HBM, HBM],
         name="split_heads",
     )(spot, qk, values)
@@ -403,11 +403,12 @@
     spot = jnp.stack([lax.axis_index("round"), lax.axis_index("seq") // PEERS]).astype(i32)
     other = lax.ppermute(dest_dev, "round", [(0, 1), (1, 0)])
     mine = {}
+    mine[1], mine[3] = split_heads(spot, qk, values, (1, 3))
+    for o in (1, 3):
+        mine[o] = hop(mine[o], o)
     (mine[2],) = split_heads(spot, qk, values, (2,))
     mine[2] = hop(mine[2], 2)
-    mine[1], mine[3], mine[0] = split_heads(spot, qk, values, (1, 3, 0))
-    for o in (1, 3):
-        mine[o] = hop(mine[o], o)
+    (mine[0],) = split_heads(spot, qk, values, (0,), 16 << 20)
     mine = [mine[o] for o in range(HOPS)]
     here = places(spot, dest_dev, other)
     spots = [here] + [hop(here, o) for o in range(1, HOPS)]
@@ -424,7 +425,7 @@
     out, lse = unpack(pos[0], back[0])
     done = {}
     done[2], done[1] = merge(pos[1], back[1], out, lse, (2, 1))
-    for o in (2, 1):
+    for o in (1, 2):
         done[o] = hop(done[o], -o)
     done[3], done[0] = merge(pos[1], back[1], out, lse, (3, 0))
     done[3] = hop(done[3], -3)

time: 184 us -> 183 us (level)
    pallas_call x2 -> x3, Pallas kernels: 5.17 us -> 5.58 us  [split_heads(): call(body, (jax.ShapeDtypeStruct((ROWS, 2 * HEAD), bf16),) * len(slots),...]
where the time goes in v3:
time: 183 us; the launch traced here: 180 us
  waiting for transfers between devices  92.5 us (51%)
  Pallas kernels  44.1 us (24%)
  starting transfers between devices  40.7 us (22%)
  local copies, waits for them, and re-layouts  2.33 us (1%)
    all_to_all x4, waiting for transfers between devices, swap(): return lax.all_to_all(x, 'seq', 0, 0, tiled=True, axis_index_groups=NEAR)  29.5 us
    ppermute x1, waiting for transfers between devices, routed(): halo = lax.ppermute(tails[0], 'seq', NEXT)  22.9 us
    ppermute x9, starting transfers between devices, hop(): lax.ppermute(x, 'seq', [(s, (s + PEERS * o) % count) for s in range(count)])  21.5 us
    ppermute x9, waiting for transfers between devices, hop(): lax.ppermute(x, 'seq', [(s, (s + PEERS * o) % count) for s in range(count)])  20.2 us
    pallas_call x2, Pallas kernels, attend(): call(attend_body, jax.ShapeDtypeStruct((PEERS, MSG_OUT, HEAD), bf16), [pl...  18.6 us
    all_to_all x4, starting transfers between devices, swap(): return lax.all_to_all(x, 'seq', 0, 0, tiled=True, axis_index_groups=NEAR)  17.9 us
    ppermute x1, waiting for transfers between devices, routed(): halo = lax.ppermute(tails[1], 'seq', NEXT)  15.3 us
    pallas_call x3, Pallas kernels, split_heads(): call(body, (jax.ShapeDtypeStruct((ROWS, 2 * HEAD), bf16),) * len(slots),...  5.58 us
  transfers between devices with their start and end apart: 16, of which 10 were waited for; matrix products, arithmetic and copies ran while one was open for 0% of the time, Pallas kernels for 19%

profile of v3, /device:TPU:4, one launch (start us, length us, event | category | flops | bytes accessed | tf_op | source)
XLA Modules:
  0.0 180.4 jit_solution(2838489128327300576)
XLA Ops:
  0.0 0.6 pad_add_fusion.spot_ref
  0.6 2.4 %split_heads.5 = bf16[512,256]{1,0:T(8,128)(2,1)} custom-call(s32[2]{0:T(128)} %pad_add_fusion.spot_ref, bf16[512,1024]{1,0:T(8,128)(2,1)} %qk_ref.5, bf16[512,1024]{1,0:T(8,128)(2,1)} %v_ref.5), custom_call_target="tpu_custom_call" | custom-call | tf_op jit(solution)/shard_map/split_heads/pallas_call | solution.py:112
  3.0 0.0 copy-start.5
  3.0 0.0 copy-start.4
  3.0 0.0 copy-start
  3.0 0.0 copy-start.1
  3.0 7.3 %collective-permute-start.1 = (bf16[512,256]{1,0:T(8,128)(2,1)}, bf16[512,256]{1,0:T(8,128)(2,1)S(1)}, u32[]{:S(2)}, u32[]{:S(2)}) collective-permute-start(bf16[512,256]{1,0:T(8,128)(2,1)} %split_heads.5), channel_id=1, source_target_pairs={{0,64},{1,65},{2,66},{3,67},{4,68},{5,69},{6,70},{7,71},{8,72},{9,... | collective-permute-start | bytes 786440 | tf_op jit(solution)/shard_map/ppermute | solution.py:391
  10.3 2.6 %split_heads.4 = (bf16[512,256]{1,0:T(8,128)(2,1)}, bf16[512,256]{1,0:T(8,128)(2,1)}) custom-call(s32[2]{0:T(128)} %pad_add_fusion.spot_ref, bf16[512,1024]{1,0:T(8,128)(2,1)} %qk_ref.5, bf16[512,1024]{1,0:T(8,128)(2,1)} %v_ref.5), custom_call_target="tpu_custom_call" | custom-call | tf_op jit(solution)/shard_map/split_heads/pallas_call | solution.py:112
  12.9 1.6 collective-permute-start
  14.4 2.7 %collective-permute-start.2 = (bf16[512,256]{1,0:T(8,128)(2,1)}, bf16[512,256]{1,0:T(8,128)(2,1)S(1)}, u32[]{:S(2)}, u32[]{:S(2)}) collective-permute-start(bf16[512,256]{1,0:T(8,128)(2,1)} %get-tuple-element.22), channel_id=1, source_target_pairs={{0,96},{1,97},{2,98},{3,99},{4,100},{5,101},{6,102},{7,103},{8,104... | collective-permute-start | bytes 786440 | tf_op jit(solution)/shard_map/ppermute | solution.py:391
  17.1 0.0 copy-done.5
  17.1 0.5 collective-permute-start.3
  17.6 4.6 %collective-permute-done.3.other_ref = s32[1,512]{1,0:T(1,128)S(1)} collective-permute-done((s32[1,512]{1,0:T(1,128)S(1)}, s32[1,512]{1,0:T(1,128)S(1)}, u32[]{:S(2)}, u32[]{:S(2)}) %collective-permute-start.3) | collective-permute-done | bytes 2080 | tf_op jit(solution)/shard_map/ppermute | solution.py:404
  22.2 0.0 copy-done.4
  22.2 1.0 places.1.refs_4_
  23.2 0.1 collective-permute-start.6
  23.3 3.8 %collective-permute-start.5 = (bf16[16,256]{1,0:T(8,128)(2,1)S(1)}, bf16[16,256]{1,0:T(8,128)(2,1)S(1)}, u32[]{:S(2)}, u32[]{:S(2)}) collective-permute-start(bf16[16,256]{1,0:T(8,128)(2,1)S(1)} %places.1.refs_4_), channel_id=1, source_target_pairs={{0,64},{1,65},{2,66},{3,67},{4,68},{5,69},{6,70},{7,71},{8,72},{9,... | collective-permute-start | bytes 24584 | tf_op jit(solution)/shard_map/ppermute | solution.py:391
  27.1 7.8 %collective-permute-done.6.refs_7_ = bf16[16,256]{1,0:T(8,128)(2,1)S(1)} collective-permute-done((bf16[16,256]{1,0:T(8,128)(2,1)S(1)}, bf16[16,256]{1,0:T(8,128)(2,1)S(1)}, u32[]{:S(2)}, u32[]{:S(2)}) %collective-permute-start.6) | collective-permute-done | bytes 8224 | tf_op jit(solution)/shard_map/ppermute | solution.py:391
  34.9 0.5 collective-permute-start.4
  35.4 0.0 copy-done
  35.4 0.0 copy-done.1
  35.4 0.6 split_heads.3.refs_0_
  36.0 0.0 collective-permute-done.5.refs_6_
  36.0 4.6 %collective-permute-done.4.refs_5_ = bf16[16,256]{1,0:T(8,128)(2,1)S(1)} collective-permute-done((bf16[16,256]{1,0:T(8,128)(2,1)S(1)}, bf16[16,256]{1,0:T(8,128)(2,1)S(1)}, u32[]{:S(2)}, u32[]{:S(2)}) %collective-permute-start.4) | collective-permute-done | bytes 8224 | tf_op jit(solution)/shard_map/ppermute | solution.py:391
  40.6 0.0 collective-permute-done.1.refs_2_
  40.6 0.0 collective-permute-done.refs_1_
  40.6 0.0 collective-permute-done.2.refs_3_
  40.6 2.5 %pack.3 = (bf16[32,96,256]{2,1,0:T(8,128)(2,1)S(1)}, s32[4,512]{1,0:T(4,128)S(1)}) custom-call(bf16[512,256]{1,0:T(8,128)(2,1)S(1)} %split_heads.3.refs_0_, bf16[512,256]{1,0:T(8,128)(2,1)S(1)} %collective-permute-done.refs_1_, bf16[512,256]{1,0:T(8,128)(2,1)S(1)} %collective-permute-done.1.refs_2_, bf16[512,256]{1,0:T(8,128)(2,1)S(1)} %collective-permute-done.2.refs_3_, ...), custom_call_target="tpu_custom_call" | custom-call | tf_op jit(solution)/shard_map/pack/pallas_call | solution.py:170
  43.2 0.0 copy-start.3
  43.2 1.1 copy-done.3
  44.3 5.5 %all-to-all-start.2 = ((bf16[32,96,256]{2,1,0:T(8,128)(2,1)}), bf16[32,96,256]{2,1,0:T(8,128)(2,1)S(1)}, u32[]{:S(2)}, u32[]{:S(2)}) async-start(bf16[32,96,256]{2,1,0:T(8,128)(2,1)} %copy-done.3), calls=%async_computation.2 | async-start | bytes 3145728 | tf_op jit(solution)/shard_map/all_to_all | solution.py:395
  49.8 2.5 %pack.2 = (bf16[32,96,256]{2,1,0:T(8,128)(2,1)S(1)}, s32[4,512]{1,0:T(4,128)S(1)}) custom-call(bf16[512,256]{1,0:T(8,128)(2,1)S(1)} %split_heads.3.refs_0_, bf16[512,256]{1,0:T(8,128)(2,1)S(1)} %collective-permute-done.refs_1_, bf16[512,256]{1,0:T(8,128)(2,1)S(1)} %collective-permute-done.1.refs_2_, bf16[512,256]{1,0:T(8,128)(2,1)S(1)} %collective-permute-done.2.refs_3_, ...), custom_call_target="tpu_custom_call" | custom-call | tf_op jit(solution)/shard_map/pack/pallas_call | solution.py:170
  52.4 0.0 copy-start.2
  52.4 1.2 copy-done.2
  53.5 17.9 %all-to-all-done.2.x_ref = bf16[32,96,256]{2,1,0:T(8,128)(2,1)S(1)} async-done(((bf16[32,96,256]{2,1,0:T(8,128)(2,1)}), bf16[32,96,256]{2,1,0:T(8,128)(2,1)S(1)}, u32[]{:S(2)}, u32[]{:S(2)}) %all-to-all-start.2) | async-done | bytes 1572896 | tf_op jit(solution)/shard_map/all_to_all | solution.py:395
  71.5 4.3 %all-to-all-start = ((bf16[32,96,256]{2,1,0:T(8,128)(2,1)}), bf16[32,96,256]{2,1,0:T(8,128)(2,1)S(1)}, u32[]{:S(2)}, u32[]{:S(2)}) async-start(bf16[32,96,256]{2,1,0:T(8,128)(2,1)} %copy-done.2), calls=%async_computation | async-start | bytes 3145728 | tf_op jit(solution)/shard_map/all_to_all | solution.py:395
  75.8 0.7 tail.3.tail_ref
  76.5 0.5 collective-permute-start.8
  77.0 1.6 compact.3
  78.6 22.9 %collective-permute-done.8.halo_ref = bf16[512,256]{1,0:T(8,128)(2,1)S(1)} collective-permute-done((bf16[512,256]{1,0:T(8,128)(2,1)S(1)}, bf16[512,256]{1,0:T(8,128)(2,1)S(1)}, u32[]{:S(2)}, u32[]{:S(2)}) %collective-permute-start.8) | collective-permute-done | bytes 262176 | tf_op jit(solution)/shard_map/ppermute | solution.py:418
  101.5 9.3 %attend.3 = bf16[32,104,128]{2,1,0:T(8,128)(2,1)} custom-call(bf16[2048,256]{1,0:T(8,128)(2,1)S(1)} %get-tuple-element.29.x_ref, bf16[512,256]{1,0:T(8,128)(2,1)S(1)} %collective-permute-done.8.halo_ref, f32[768,128]{1,0:T(8,128)S(1)} %get-tuple-element.30.tcol_ref), custom_call_target="tpu_custom_call" | custom-call | tf_op jit(solution)/shard_map/attend/pallas_call | solution.py:289
  110.8 0.0 all-to-all-done.x_ref
  110.8 3.9 %all-to-all-start.3 = ((bf16[32,104,128]{2,1,0:T(8,128)(2,1)}), bf16[32,104,128]{2,1,0:T(8,128)(2,1)S(1)}, u32[]{:S(2)}, u32[]{:S(2)}) async-start(bf16[32,104,128]{2,1,0:T(8,128)(2,1)} %attend.3), calls=%async_computation.3 | async-start | bytes 1703936 | tf_op jit(solution)/shard_map/all_to_all | solution.py:395
  114.7 0.7 tail.2.tail_ref
  115.4 0.2 collective-permute-start.7
  115.6 1.6 compact.2
  117.3 15.3 %collective-permute-done.7.halo_ref = bf16[512,256]{1,0:T(8,128)(2,1)S(1)} collective-permute-done((bf16[512,256]{1,0:T(8,128)(2,1)S(1)}, bf16[512,256]{1,0:T(8,128)(2,1)S(1)}, u32[]{:S(2)}, u32[]{:S(2)}) %collective-permute-start.7) | collective-permute-done | bytes 262176 | tf_op jit(solution)/shard_map/ppermute | solution.py:422
  132.6 9.3 %attend.2 = bf16[32,104,128]{2,1,0:T(8,128)(2,1)} custom-call(bf16[2048,256]{1,0:T(8,128)(2,1)S(1)} %get-tuple-element.25.x_ref, bf16[512,256]{1,0:T(8,128)(2,1)S(1)} %collective-permute-done.7.halo_ref, f32[768,128]{1,0:T(8,128)S(1)} %get-tuple-element.26.tcol_ref), custom_call_target="tpu_custom_call" | custom-call | tf_op jit(solution)/shard_map/attend/pallas_call | solution.py:289
  141.9 0.0 all-to-all-done.3.x_ref
  141.9 4.1 %all-to-all-start.1 = ((bf16[32,104,128]{2,1,0:T(8,128)(2,1)}), bf16[32,104,128]{2,1,0:T(8,128)(2,1)S(1)}, u32[]{:S(2)}, u32[]{:S(2)}) async-start(bf16[32,104,128]{2,1,0:T(8,128)(2,1)} %attend.2), calls=%async_computation.1 | async-start | bytes 1703936 | tf_op jit(solution)/shard_map/all_to_all | solution.py:395
  146.1 2.5 %unpack.1 = (bf16[4,512,128]{2,1,0:T(8,128)(2,1)S(1)}, f32[512,128]{1,0:T(8,128)S(1)}) custom-call(s32[4,512]{1,0:T(4,128)S(1)} %get-tuple-element.27.pos_ref, bf16[32,104,128]{2,1,0:T(8,128)(2,1)S(1)} %all-to-all-done.3.x_ref), custom_call_target="tpu_custom_call" | custom-call | tf_op jit(solution)/shard_map/unpack/pallas_call | solution.py:342
  148.5 11.6 %all-to-all-done.1.x_ref = bf16[32,104,128]{2,1,0:T(8,128)(2,1)S(1)} async-done(((bf16[32,104,128]{2,1,0:T(8,128)(2,1)}), bf16[32,104,128]{2,1,0:T(8,128)(2,1)S(1)}, u32[]{:S(2)}, u32[]{:S(2)}) %all-to-all-start.1) | async-done | bytes 852000 | tf_op jit(solution)/shard_map/all_to_all | solution.py:395
  160.1 2.7 %merge.3 = (bf16[512,128]{1,0:T(8,128)(2,1)S(1)}, bf16[512,128]{1,0:T(8,128)(2,1)S(1)}) custom-call(s32[4,512]{1,0:T(4,128)S(1)} %get-tuple-element.23.pos_ref, bf16[32,104,128]{2,1,0:T(8,128)(2,1)S(1)} %all-to-all-done.1.x_ref, bf16[4,512,128]{2,1,0:T(8,128)(2,1)S(1)} %get-tuple-element.31.other_ref, f32[512,128]{1,0:T(8,128)S(1)} %get-tuple-element.32.other_lse_ref), custom_call_target="tpu_custom_call" | custom-call | tf_op jit(solution)/shard_map/merge/pallas_call | solution.py:360
  162.8 2.6 %collective-permute-start.9 = (bf16[512,128]{1,0:T(8,128)(2,1)S(1)}, bf16[512,128]{1,0:T(8,128)(2,1)S(1)}, u32[]{:S(2)}, u32[]{:S(2)}) collective-permute-start(bf16[512,128]{1,0:T(8,128)(2,1)S(1)} %get-tuple-element.34), channel_id=1, source_target_pairs={{0,96},{1,97},{2,98},{3,99},{4,100},{5,101},{6,102},{7,103},{8,104... | collective-permute-start | bytes 393224 | tf_op jit(solution)/shard_map/ppermute | solution.py:391
  165.4 0.3 collective-permute-start.10
  165.8 2.7 %merge.2 = (bf16[512,128]{1,0:T(8,128)(2,1)S(1)}, bf16[512,128]{1,0:T(8,128)(2,1)S(1)}) custom-call(s32[4,512]{1,0:T(4,128)S(1)} %get-tuple-element.23.pos_ref, bf16[32,104,128]{2,1,0:T(8,128)(2,1)S(1)} %all-to-all-done.1.x_ref, bf16[4,512,128]{2,1,0:T(8,128)(2,1)S(1)} %get-tuple-element.31.other_ref, f32[512,128]{1,0:T(8,128)S(1)} %get-tuple-element.32.other_lse_ref), custom_call_target="tpu_custom_call" | custom-call | tf_op jit(solution)/shard_map/merge/pallas_call | solution.py:360
  168.4 2.7 %collective-permute-start.11 = (bf16[512,128]{1,0:T(8,128)(2,1)S(1)}, bf16[512,128]{1,0:T(8,128)(2,1)S(1)}, u32[]{:S(2)}, u32[]{:S(2)}) collective-permute-start(bf16[512,128]{1,0:T(8,128)(2,1)S(1)} %get-tuple-element.36), channel_id=1, source_target_pairs={{0,32},{1,33},{2,34},{3,35},{4,36},{5,37},{6,38},{7,39},{8,40},{9,... | collective-permute-start | bytes 393224 | tf_op jit(solution)/shard_map/ppermute | solution.py:391
  171.1 1.3 collective-permute-done.9.refs_1_
  172.5 5.3 %collective-permute-done.10.refs_2_ = bf16[512,128]{1,0:T(8,128)(2,1)S(1)} collective-permute-done((bf16[512,128]{1,0:T(8,128)(2,1)S(1)}, bf16[512,128]{1,0:T(8,128)(2,1)S(1)}, u32[]{:S(2)}, u32[]{:S(2)}) %collective-permute-start.10) | collective-permute-done | bytes 131104 | tf_op jit(solution)/shard_map/ppermute | solution.py:391
  177.8 1.2 collective-permute-done.11.refs_3_
  178.9 1.4 join_heads.1
Async XLA Ops:
  3.0 14.1 %copy-start.5 = (s32[1,512]{1,0:T(1,128)S(1)}, s32[1,512]{1,0:T(1,128)}, u32[]{:S(2)}) copy-start(s32[1,512]{1,0:T(1,128)} %own_ref.1) | copy-start | bytes 6148
  3.0 19.2 %copy-start.4 = (s32[2]{0:T(128)S(1)}, s32[2]{0:T(128)}, u32[]{:S(2)}) copy-start(s32[2]{0:T(128)} %pad_add_fusion.spot_ref) | copy-start | bytes 28
  3.0 32.4 %copy-start = (bf16[512,1024]{1,0:T(8,128)(2,1)S(1)}, bf16[512,1024]{1,0:T(8,128)(2,1)}, u32[]{:S(2)}) copy-start(bf16[512,1024]{1,0:T(8,128)(2,1)} %qk_ref.5) | copy-start | bytes 3145732
  3.0 32.4 %copy-start.1 = (bf16[512,1024]{1,0:T(8,128)(2,1)S(1)}, bf16[512,1024]{1,0:T(8,128)(2,1)}, u32[]{:S(2)}) copy-start(bf16[512,1024]{1,0:T(8,128)(2,1)} %v_ref.5) | copy-start | bytes 3145732
  3.0 37.6 %collective-permute-start.1 = (bf16[512,256]{1,0:T(8,128)(2,1)}, bf16[512,256]{1,0:T(8,128)(2,1)S(1)}, u32[]{:S(2)}, u32[]{:S(2)}) collective-permute-start(bf16[512,256]{1,0:T(8,128)(2,1)} %split_heads.5), channel_id=1, source_target_pairs={{0,64},{1,65},{2,66},{3,67},{4,68},{5,69},{6,70},{7,71},{8,72},{9,... | collective-permute-start | bytes 786440 | tf_op jit(solution)/shard_map/ppermute | solution.py:391
  12.9 27.8 %collective-permute-start = (bf16[512,256]{1,0:T(8,128)(2,1)}, bf16[512,256]{1,0:T(8,128)(2,1)S(1)}, u32[]{:S(2)}, u32[]{:S(2)}) collective-permute-start(bf16[512,256]{1,0:T(8,128)(2,1)} %get-tuple-element.21), channel_id=1, source_target_pairs={{0,32},{1,33},{2,34},{3,35},{4,36},{5,37},{6,38},{7,39},{8,40},{9,... | collective-permute-start | bytes 786440 | tf_op jit(solution)/shard_map/ppermute | solution.py:391
  14.4 26.2 %collective-permute-start.2 = (bf16[512,256]{1,0:T(8,128)(2,1)}, bf16[512,256]{1,0:T(8,128)(2,1)S(1)}, u32[]{:S(2)}, u32[]{:S(2)}) collective-permute-start(bf16[512,256]{1,0:T(8,128)(2,1)} %get-tuple-element.22), channel_id=1, source_target_pairs={{0,96},{1,97},{2,98},{3,99},{4,100},{5,101},{6,102},{7,103},{8,104... | collective-permute-start | bytes 786440 | tf_op jit(solution)/shard_map/ppermute | solution.py:391
  17.1 5.1 %collective-permute-start.3 = (s32[1,512]{1,0:T(1,128)S(1)}, s32[1,512]{1,0:T(1,128)S(1)}, u32[]{:S(2)}, u32[]{:S(2)}) collective-permute-start(s32[1,512]{1,0:T(1,128)S(1)} %copy-done.5), channel_id=1, source_target_pairs={{0,128},{128,0},{1,129},{129,1},{2,130},{130,2},{3,131},{131,3},{4... | collective-permute-start | bytes 6152 | tf_op jit(solution)/shard_map/ppermute | solution.py:404
  23.2 11.7 %collective-permute-start.6 = (bf16[16,256]{1,0:T(8,128)(2,1)S(1)}, bf16[16,256]{1,0:T(8,128)(2,1)S(1)}, u32[]{:S(2)}, u32[]{:S(2)}) collective-permute-start(bf16[16,256]{1,0:T(8,128)(2,1)S(1)} %places.1.refs_4_), channel_id=1, source_target_pairs={{0,96},{1,97},{2,98},{3,99},{4,100},{5,101},{6,102},{7,103},{8,104... | collective-permute-start | bytes 24584 | tf_op jit(solution)/shard_map/ppermute | solution.py:391
  23.3 12.8 %collective-permute-start.5 = (bf16[16,256]{1,0:T(8,128)(2,1)S(1)}, bf16[16,256]{1,0:T(8,128)(2,1)S(1)}, u32[]{:S(2)}, u32[]{:S(2)}) collective-permute-start(bf16[16,256]{1,0:T(8,128)(2,1)S(1)} %places.1.refs_4_), channel_id=1, source_target_pairs={{0,64},{1,65},{2,66},{3,67},{4,68},{5,69},{6,70},{7,71},{8,72},{9,... | collective-permute-start | bytes 24584 | tf_op jit(solution)/shard_map/ppermute | solution.py:391
  34.9 5.8 %collective-permute-start.4 = (bf16[16,256]{1,0:T(8,128)(2,1)S(1)}, bf16[16,256]{1,0:T(8,128)(2,1)S(1)}, u32[]{:S(2)}, u32[]{:S(2)}) collective-permute-start(bf16[16,256]{1,0:T(8,128)(2,1)S(1)} %places.1.refs_4_), channel_id=1, source_target_pairs={{0,32},{1,33},{2,34},{3,35},{4,36},{5,37},{6,38},{7,39},{8,40},{9,... | collective-permute-start | bytes 24584 | tf_op jit(solution)/shard_map/ppermute | solution.py:391
  43.2 1.1 copy-start.3
  44.3 27.2 %all-to-all-start.2 = ((bf16[32,96,256]{2,1,0:T(8,128)(2,1)}), bf16[32,96,256]{2,1,0:T(8,128)(2,1)S(1)}, u32[]{:S(2)}, u32[]{:S(2)}) async-start(bf16[32,96,256]{2,1,0:T(8,128)(2,1)} %copy-done.3), calls=%async_computation.2 | async-start | bytes 3145728 | tf_op jit(solution)/shard_map/all_to_all | solution.py:395
  52.4 1.2 copy-start.2
  71.5 39.3 %all-to-all-start = ((bf16[32,96,256]{2,1,0:T(8,128)(2,1)}), bf16[32,96,256]{2,1,0:T(8,128)(2,1)S(1)}, u32[]{:S(2)}, u32[]{:S(2)}) async-start(bf16[32,96,256]{2,1,0:T(8,128)(2,1)} %copy-done.2), calls=%async_computation | async-start | bytes 3145728 | tf_op jit(solution)/shard_map/all_to_all | solution.py:395
  76.5 25.0 %collective-permute-start.8 = (bf16[512,256]{1,0:T(8,128)(2,1)S(1)}, bf16[512,256]{1,0:T(8,128)(2,1)S(1)}, u32[]{:S(2)}, u32[]{:S(2)}) collective-permute-start(bf16[512,256]{1,0:T(8,128)(2,1)S(1)} %tail.3.tail_ref), channel_id=1, source_target_pairs={{0,1},{1,2},{2,3},{3,4},{4,5},{5,6},{6,7},{7,8},{8,9},{9,10},{10,1... | collective-permute-start | bytes 786440 | tf_op jit(solution)/shard_map/ppermute | solution.py:418
  110.8 31.1 %all-to-all-start.3 = ((bf16[32,104,128]{2,1,0:T(8,128)(2,1)}), bf16[32,104,128]{2,1,0:T(8,128)(2,1)S(1)}, u32[]{:S(2)}, u32[]{:S(2)}) async-start(bf16[32,104,128]{2,1,0:T(8,128)(2,1)} %attend.3), calls=%async_computation.3 | async-start | bytes 1703936 | tf_op jit(solution)/shard_map/all_to_all | solution.py:395
  115.4 17.2 %collective-permute-start.7 = (bf16[512,256]{1,0:T(8,128)(2,1)S(1)}, bf16[512,256]{1,0:T(8,128)(2,1)S(1)}, u32[]{:S(2)}, u32[]{:S(2)}) collective-permute-start(bf16[512,256]{1,0:T(8,128)(2,1)S(1)} %tail.2.tail_ref), channel_id=1, source_target_pairs={{0,1},{1,2},{2,3},{3,4},{4,5},{5,6},{6,7},{7,8},{8,9},{9,10},{10,1... | collective-permute-start | bytes 786440 | tf_op jit(solution)/shard_map/ppermute | solution.py:422
  141.9 18.2 %all-to-all-start.1 = ((bf16[32,104,128]{2,1,0:T(8,128)(2,1)}), bf16[32,104,128]{2,1,0:T(8,128)(2,1)S(1)}, u32[]{:S(2)}, u32[]{:S(2)}) async-start(bf16[32,104,128]{2,1,0:T(8,128)(2,1)} %attend.2), calls=%async_computation.1 | async-start | bytes 1703936 | tf_op jit(solution)/shard_map/all_to_all | solution.py:395
  162.8 9.6 %collective-permute-start.9 = (bf16[512,128]{1,0:T(8,128)(2,1)S(1)}, bf16[512,128]{1,0:T(8,128)(2,1)S(1)}, u32[]{:S(2)}, u32[]{:S(2)}) collective-permute-start(bf16[512,128]{1,0:T(8,128)(2,1)S(1)} %get-tuple-element.34), channel_id=1, source_target_pairs={{0,96},{1,97},{2,98},{3,99},{4,100},{5,101},{6,102},{7,103},{8,104... | collective-permute-start | bytes 393224 | tf_op jit(solution)/shard_map/ppermute | solution.py:391
  165.4 12.4 %collective-permute-start.10 = (bf16[512,128]{1,0:T(8,128)(2,1)S(1)}, bf16[512,128]{1,0:T(8,128)(2,1)S(1)}, u32[]{:S(2)}, u32[]{:S(2)}) collective-permute-start(bf16[512,128]{1,0:T(8,128)(2,1)S(1)} %get-tuple-element.35), channel_id=1, source_target_pairs={{0,64},{1,65},{2,66},{3,67},{4,68},{5,69},{6,70},{7,71},{8,72},{9,... | collective-permute-start | bytes 393224 | tf_op jit(solution)/shard_map/ppermute | solution.py:391
  168.4 10.5 %collective-permute-start.11 = (bf16[512,128]{1,0:T(8,128)(2,1)S(1)}, bf16[512,128]{1,0:T(8,128)(2,1)S(1)}, u32[]{:S(2)}, u32[]{:S(2)}) collective-permute-start(bf16[512,128]{1,0:T(8,128)(2,1)S(1)} %get-tuple-element.36), channel_id=1, source_target_pairs={{0,32},{1,33},{2,34},{3,35},{4,36},{5,37},{6,38},{7,39},{8,40},{9,... | collective-permute-start | bytes 393224 | tf_op jit(solution)/shard_map/ppermute | solution.py:391
